TPU v7x, 32 devices: a whole 2x2x4 slice. The times are simulated.
32 devices in a mesh: sample: 4 (over y, x), gz: 8 (over z, core).
Axes of the slice: x: 2, y: 2, z: 4, core: 2. Of those that a mesh axis runs over, the one named last changes fastest.
Arguments:
- field_now: float32 [12, 16, 160, 256], P('sample', 'gz'), parts along dimension 0, may hold values from -6 to 6
- field_before: float32 [12, 16, 160, 256], P('sample', 'gz'), parts along dimension 0, may hold values from -6 to 6
- lame_lambda: float32 [16, 640, 256], P('gz', 'sample'), parts along dimension 1, may hold values from 0.5 to 1.5
- shear_modulus: float32 [16, 640, 256], P('gz', 'sample'), parts along dimension 1, may hold values from 0.5 to 1.5
- density: float32 [16, 640, 256], P('gz', 'sample'), parts along dimension 1, may hold values from 1 to 2
- source_field: float32 [12, 16, 160, 256], P('sample', 'gz'), parts along dimension 0, may hold values from -6 to 6
- wavelet: float32 [32], P('sample'), parts along dimension 0, may hold values from -4 to 4
- prior_mean: float32 [16, 640, 256], P('gz', 'sample'), parts along dimension 1, may hold values from 0.5 to 1.5
- steps_taken: float32 [16, 16, 160, 256], P('sample', 'gz'), parts along dimension 0
- grad_change: float32 [16, 16, 160, 256], P('sample', 'gz'), parts along dimension 0, as said below
Outputs:
- field_final: float32 [12, 16, 160, 256], P('sample', 'gz'), parts along dimension 0
- gradient: float32 [16, 640, 256], P('gz', 'sample'), parts along dimension 1
- direction: float32 [16, 640, 256], P('gz', 'sample'), parts along dimension 1
There are 4 independent parts, one for each index of `sample`. A program takes and returns all parts, laid end to end along the dimension named above; each array names one. Nothing has to cross between parts.
Inputs may be any that keep to these rules, and one draw needn't show every extreme that they name: Each entry of grad_change is 0.5 to 2 times the matching entry of steps_taken.
All inputs are finite; a program needn't handle non-finite values.
Results may differ from a plain program's by a relative error of at most 0.0003.
Values sent between devices are 32-bit elements; how exact they have to be, the bound alone decides.
No kernel may reach another device: no remote copies, remote signals or barrier semaphores. Data moves between devices by JAX's collectives and lax.ppermute only.
A program may use at most 64 MiB of HBM per device.

v0:
```python
import functools

import jax
import jax.numpy as jnp
from jax import lax
from jax.experimental import pallas as pl
from jax.experimental.pallas import tpu as pltpu
from jax.sharding import PartitionSpec as P

STEPS = 8
PAIRS = 4
ROWS = 8
LANES = 128
AXES = ("sample", "gz")
DOTS = [("s", i, j) for i in range(PAIRS) for j in range(i, PAIRS)] + [
    ("y", i, j) for i in range(PAIRS) for j in range(i, PAIRS)
]
DOT_ROWS = 32

VMEM = pl.BlockSpec(memory_space=pltpu.VMEM)
SMEM = pl.BlockSpec(memory_space=pltpu.SMEM)


def mul(x, y):
    return [a * b for a, b in zip(x, y)]


def add(x, y):
    return [a + b for a, b in zip(x, y)]


def sub(x, y):
    return [a - b for a, b in zip(x, y)]


def scale(x, factor):
    return [a * factor for a in x]


def lanes_of(ref, index, tile):
    row = tile * ROWS if isinstance(tile, int) else pl.multiple_of(tile * ROWS, ROWS)
    count = ref.shape[-1] // LANES
    return [ref[(*index, pl.ds(row, ROWS), pl.ds(k * LANES, LANES))] for k in range(count)]


def store(ref, index, tile, values):
    row = tile * ROWS if isinstance(tile, int) else pl.multiple_of(tile * ROWS, ROWS)
    for k, value in enumerate(values):
        ref[(*index, pl.ds(row, ROWS), pl.ds(k * LANES, LANES))] = value


def along_y(x, lane):
    up = [pltpu.roll(a, LANES - 1, 1) for a in x]
    down = [pltpu.roll(a, 1, 1) for a in x]
    count = len(x)
    zero = jnp.zeros_like(x[0])
    high = [
        jnp.where(lane == LANES - 1, up[k + 1] if k + 1 < count else zero, up[k])
        for k in range(count)
    ]
    low = [jnp.where(lane == 0, down[k - 1] if k > 0 else zero, down[k]) for k in range(count)]
    return high, low


def along_x(before, here, after, row, first, last):
    high, low = [], []
    for b, h, a in zip(before, here, after):
        high.append(
            jnp.where(row == ROWS - 1, pltpu.roll(a, ROWS - 1, 0) * last, pltpu.roll(h, ROWS - 1, 0))
        )
        low.append(jnp.where(row == 0, pltpu.roll(b, 1, 0) * first, pltpu.roll(h, 1, 0)))
    return high, low


def plane_update(centre, ici, d2d, quarter, row, lane, first, last):
    u = [[centre(c, k) for k in (-1, 0, 1)] for c in range(3)]
    i0, d0 = [ici(c, 0) for c in range(3)], [d2d(c, 0) for c in range(3)]
    w = [scale(sub(i0[c], d0[c]), quarter) for c in range(3)]
    w1 = [scale(sub(ici(1, k), d2d(1, k)), quarter) if k else w[1] for k in (-1, 0, 1)]
    w0 = [scale(sub(ici(0, k), d2d(0, k)), quarter) if k else w[0] for k in (-1, 0, 1)]
    y2 = [along_y(u[2][k], lane) for k in range(3)]
    g1 = [add(w0[k], scale(sub(*y2[k]), 0.25)) for k in range(3)]
    xs = [along_x(*u[c], row, first, last) for c in range(3)]
    ys = [along_y(u[0][1], lane), along_y(u[1][1], lane), y2[1]]
    xw1 = along_x(*w1, row, first, last)
    xg1 = along_x(*g1, row, first, last)
    yw2 = along_y(w[2], lane)
    g2 = add(w[0], scale(sub(*xs[1]), 0.25))
    yg2 = along_y(g2, lane)
    twice = [scale(u[c][1], 2.0) for c in range(3)]
    second = [
        [
            sub(add(i0[c], d0[c]), twice[c]),
            sub(add(*xs[c]), twice[c]),
            sub(add(*ys[c]), twice[c]),
        ]
        for c in range(3)
    ]
    lap = [add(add(second[c][0], second[c][1]), second[c][2]) for c in range(3)]
    grad_div = [
        add(second[0][0], add(sub(*xw1), sub(*yw2))),
        add(second[1][1], sub(*xg1)),
        add(second[2][2], sub(*yg2)),
    ]
    return [u[c][1] for c in range(3)], twice, grad_div, lap


def step_kernel(step, start, stop, total, splits, parts, ip, fs, *refs):
    names = ["h", "q", "p", "f", "pb", "fb"] + ([] if step == 0 else ["corr"])
    source = {}
    at = 0
    for name in names:
        source[name] = refs[at : at + parts]
        at += parts
    ca, cb, cf, src = refs[at : at + 4]
    p_out, f_out, corr_out = refs[at + 4 :]
    near = ip[0]
    quarter = fs[0]
    present = fs[1]
    wave = fs[2 + step]
    row = lax.broadcasted_iota(jnp.int32, (ROWS, LANES), 0)
    lane = lax.broadcasted_iota(jnp.int32, (ROWS, LANES), 1)

    def tile_body(t, static):
        if static:
            first = 0.0 if t == 0 else 1.0
            last = 0.0 if t == total - 1 else 1.0
        else:
            first = jnp.where(t == 0, 0.0, 1.0)
            last = jnp.where(t == total - 1, 0.0, 1.0)

        def read(name, index, k):
            n = t + k
            n = min(max(n, 0), total - 1) if static else jnp.clip(n, 0, total - 1)
            held = source[name]
            if parts == 1:
                return lanes_of(held[0], index, n)
            if static and n < splits[name]:
                return lanes_of(held[0], index, n)
            return lanes_of(held[1], index, n - splits[name])

        def reader(name):
            if name == "h":
                return lambda c, k: scale(read("h", (c,), k), present)
            return lambda c, k: read(name, (c,), k)

        work = ((near, 0, "phf", "pb", p_out), (1 - near, 1, "fpq", "fb", f_out))
        for index, slot, three, older, out in work:
            centre, ici, d2d = (reader(name) for name in three)
            here, twice, grad_div, lap = plane_update(
                centre, ici, d2d, quarter, row, lane, first, last
            )
            a, b = lanes_of(ca, (index,), t), lanes_of(cb, (index,), t)
            force = scale(lanes_of(cf, (index,), t), wave)
            product = None if step == 0 else read("corr", (slot,), 0)
            for c in range(3):
                term = mul(here[c], lap[c])
                product = term if product is None else add(product, term)
                new = sub(twice[c], read(older, (c,), 0))
                new = add(new, mul(force, lanes_of(src, (c, index), t)))
                new = add(new, add(mul(a, grad_div[c]), mul(b, lap[c])))
                store(out, (c,), t - start, new)
            store(corr_out, (slot,), t - start, product)

    begin = start
    if parts == 2:
        begin = min(max(splits.values()), stop)
        for t in range(start, begin):
            tile_body(t, True)
    if begin < stop:

        def loop(t, carry):
            tile_body(t, False)
            return carry

        lax.fori_loop(begin, stop, loop, 0)


def step_call(step, start, stop, total, splits, ints, floats, held, fixed, name):
    operands = [ints, floats] + held + fixed
    cols = held[0].shape[-1]
    rows = (stop - start) * ROWS
    names = 6 if step == 0 else 7
    return call(
        functools.partial(step_kernel, step, start, stop, total, splits, len(held) // names),
        [(3, rows, cols), (3, rows, cols), (2, rows, cols)],
        operands,
        rows * cols * 240,
        name,
        2,
    )


VMEM_LIMIT = 20 * 2**20


def split_kernel(cut, ip, u, *outs):
    near = ip[0]
    rows = u.shape[2]
    for index, (low, high) in ((near, outs[:2]), (1 - near, outs[2:])):
        for c in range(3):
            low[c] = u[c, index, pl.ds(0, cut), :]
            high[c] = u[c, index, pl.ds(cut, rows - cut), :]


def join_kernel(ip, p_low, p_high, f_low, f_high, out):
    near = ip[0]
    cut, rest = p_low.shape[1], p_high.shape[1]
    for index, low, high in ((near, p_low, p_high), (1 - near, f_low, f_high)):
        for c in range(3):
            out[c, index, pl.ds(0, cut), :] = low[c]
            out[c, index, pl.ds(cut, rest), :] = high[c]


def coeff_kernel(lam, mu, rho, ca, cb, cf):
    rows = lam.shape[1] // ROWS

    def loop(t, carry):
        r = pl.ds(pl.multiple_of(t * ROWS, ROWS), ROWS)
        for d in range(lam.shape[0]):
            coeff = 0.04 / rho[d, r, :]
            m = mu[d, r, :]
            ca[d, r, :] = coeff * (lam[d, r, :] + m)
            cb[d, r, :] = coeff * m
            cf[d, r, :] = coeff
        return carry

    lax.fori_loop(0, rows, loop, 0)


def dots_kernel(s, y, out):
    depth, rows, cols = s.shape[1:]
    count = len(DOTS)

    def loop(t, sums):
        r = pl.ds(pl.multiple_of(t * ROWS, ROWS), ROWS)
        sums = list(sums)
        for d in range(depth):
            for k in range(cols // LANES):
                at = (d, r, pl.ds(k * LANES, LANES))
                vs = [s[(i, *at)] for i in range(PAIRS)]
                vy = [y[(i, *at)] for i in range(PAIRS)]
                for n, (kind, i, j) in enumerate(DOTS):
                    sums[n] = sums[n] + (vs[i] if kind == "s" else vy[i]) * vy[j]
        return tuple(sums)

    zero = jnp.zeros((ROWS, LANES), jnp.float32)
    sums = lax.fori_loop(0, rows // ROWS, loop, (zero,) * count)
    out[...] = jnp.zeros(out.shape, jnp.float32)
    for n in range(count):
        out[pl.ds(n, 1), :] = jnp.sum(sums[n], axis=0, keepdims=True)


def gradient_kernel(ip, corr_low, corr_high, mu, prior, s, y, static, grad, out):
    near = ip[0]
    cols = mu.shape[2]
    sums = (jnp.zeros((ROWS, LANES), jnp.float32),) * (2 * PAIRS)
    base = 0
    for corr in (corr_low, corr_high):

        def loop(t, sums, corr=corr, base=base):
            sums = list(sums)
            r = pl.ds(pl.multiple_of((base + t) * ROWS, ROWS), ROWS)
            r_corr = pl.ds(pl.multiple_of(t * ROWS, ROWS), ROWS)
            for slot, index in ((0, near), (1, 1 - near)):
                for k in range(cols // LANES):
                    lanes = pl.ds(k * LANES, LANES)
                    at = (index, r, lanes)
                    g = (mu[at] - prior[at]) + 0.02 * corr[slot, r_corr, lanes]
                    grad[at] = g
                    for i in range(PAIRS):
                        sums[i] = sums[i] + s[(i, *at)] * g
                        sums[PAIRS + i] = sums[PAIRS + i] + y[(i, *at)] * g
            return tuple(sums)

        tiles = corr.shape[1] // ROWS
        sums = lax.fori_loop(0, tiles, loop, sums)
        base += tiles
    out[...] = static[...]
    for n in range(2 * PAIRS):
        out[pl.ds(len(DOTS) + n, 1), :] = jnp.sum(sums[n], axis=0, keepdims=True)


def direction_kernel(parts, grad, s, y, out):
    depth, rows, cols = grad.shape
    dots = parts[0]
    for n in range(1, parts.shape[0]):
        dots = dots + parts[n]
    shift = LANES // 2
    while shift:
        dots = dots + pltpu.roll(dots, shift, 1)
        shift //= 2
    value = {}
    for n, key in enumerate(DOTS):
        value[key] = dots[n : n + 1, :]
    for i in range(PAIRS):
        value["sg", i] = dots[len(DOTS) + i : len(DOTS) + i + 1, :]
        value["yg", i] = dots[len(DOTS) + PAIRS + i : len(DOTS) + PAIRS + i + 1, :]
    rho = [1.0 / value["s", i, i] for i in range(PAIRS)]
    alpha = [None] * PAIRS
    for i in reversed(range(PAIRS)):
        inner = value["sg", i]
        for j in range(i + 1, PAIRS):
            inner = inner - alpha[j] * value["s", i, j]
        alpha[i] = rho[i] * inner
    last = PAIRS - 1
    gamma = value["s", last, last] / value["y", last, last]
    step = [None] * PAIRS
    for i in range(PAIRS):
        inner = value["yg", i]
        for j in range(PAIRS):
            inner = inner - alpha[j] * value["y", min(i, j), max(i, j)]
        inner = gamma * inner
        for j in range(i):
            inner = inner + step[j] * value["s", j, i]
        step[i] = alpha[i] - rho[i] * inner
    wide = lambda x: jnp.broadcast_to(x, (ROWS, LANES))
    by_g = wide(-gamma)
    by_y = [wide(gamma * a) for a in alpha]
    by_s = [wide(-b) for b in step]

    def loop(t, carry):
        r = pl.ds(pl.multiple_of(t * ROWS, ROWS), ROWS)
        for d in range(depth):
            for k in range(cols // LANES):
                at = (d, r, pl.ds(k * LANES, LANES))
                total = by_g * grad[at]
                for i in range(PAIRS):
                    total = total + by_y[i] * y[(i, *at)] + by_s[i] * s[(i, *at)]
                out[at] = total
        return carry

    lax.fori_loop(0, rows // ROWS, loop, 0)


def call(kernel, out_shape, operands, flops, name, smem=0):
    return pl.pallas_call(
        kernel,
        out_shape=[jax.ShapeDtypeStruct(x, jnp.float32) for x in out_shape],
        in_specs=[SMEM] * smem + [VMEM] * (len(operands) - smem),
        out_specs=[VMEM] * len(out_shape),
        compiler_params=pltpu.CompilerParams(vmem_limit_bytes=VMEM_LIMIT),
        cost_estimate=pl.CostEstimate(flops=flops, bytes_accessed=0, transcendentals=0),
        name=name,
    )(*operands)


def pairings():
    samples, count = lax.axis_size("sample"), lax.axis_size("gz")
    inside = [(i, i ^ 1) for i in range(count)]
    across = []
    for sample in range(samples):
        for i in range(1, count - 1, 2):
            across += [(sample * count + i, sample * count + i + 1)]
            across += [(sample * count + i + 1, sample * count + i)]
        partner = sample ^ 1 if samples % 2 == 0 else sample
        for i in (0, count - 1):
            across.append((sample * count + i, partner * count + i))
    return inside, across


def sum_over_gz(part):
    count = lax.axis_size("gz")
    pair = part + lax.ppermute(part, "gz", [(i, i ^ 1) for i in range(count)])
    if count > 8:
        return lax.psum(part, "gz")[None]
    parts = [pair]
    for k in range(1, count // 2):
        parts.append(lax.ppermute(pair, "gz", [(i, (i + 2 * k) % count) for i in range(count)]))
    return jnp.stack(parts)


def on_device(
    field_now,
    field_before,
    lame_lambda,
    shear_modulus,
    density,
    source_field,
    wavelet,
    prior_mean,
    steps_taken,
    grad_change,
):
    depth, rows, cols = shear_modulus.shape
    count = lax.axis_size("gz")
    assert depth == 2 and count % 2 == 0
    inside, across = pairings()
    total = rows // ROWS
    cells = shear_modulus.size
    cuts = [total // 2 + STEPS // 2 - n for n in range(STEPS + 1)]
    place = lax.axis_index("gz")
    near = place % 2
    ints = jnp.reshape(near, (1,)).astype(jnp.int32)
    sign = jnp.where(near == 1, 0.25, -0.25)
    present = jnp.where((place == 0) | (place == count - 1), 0.0, 1.0)
    floats = jnp.concatenate([jnp.stack([sign, present]).astype(jnp.float32), wavelet])

    def cut_planes(field, tiles, name):
        cut = tiles * ROWS
        shapes = [(3, cut, cols), (3, rows - cut, cols)] * 2
        outs = call(functools.partial(split_kernel, cut), shapes, [ints, field], cells, name, 1)
        return outs[:2], outs[2:]

    now = cut_planes(field_now, cuts[0], "cut_now")
    older = cut_planes(field_before, cuts[0] + 1, "cut_before")
    fixed = call(
        coeff_kernel,
        [shear_modulus.shape] * 3,
        [lame_lambda, shear_modulus, density],
        cells * 10,
        "coeffs",
    )
    fixed = list(fixed) + [source_field]
    (static,) = call(
        dots_kernel, [(DOT_ROWS, LANES)], [steps_taken, grad_change], cells * 40, "static_dots"
    )
    swap_b = lambda x: lax.ppermute(x, AXES, across)
    swap_a = lambda x: lax.ppermute(x, "gz", inside)
    ghosts = [[swap_b(now[0][i]), swap_a(now[1][i])] for i in range(2)]
    ghosts = list(zip(*ghosts))
    corr = None
    for n in range(STEPS):
        last = n == STEPS - 1
        middle = cuts[n + 1]
        groups = [*ghosts, *now, *older] + ([] if n == 0 else [corr])
        splits = {k: cuts[n] for k in ("h", "q", "p", "f", "corr")}
        splits |= {k: cuts[n] + 1 for k in ("pb", "fb")}
        args = (ints, floats)
        p_low, f_low, corr_low = step_call(
            n, 0, middle, total, splits, *args, [g[0] for g in groups], fixed, f"step{n}_low"
        )
        if not last:
            low_ghosts = [swap_b(p_low), swap_a(f_low)]
        both = [x for g in groups for x in g]
        p_high, f_high, corr_high = step_call(
            n, middle, total, total, splits, *args, both, fixed, f"step{n}_high"
        )
        if not last:
            ghosts = list(zip(low_ghosts, [swap_b(p_high), swap_a(f_high)]))
        older, now = now, ((p_low, p_high), (f_low, f_high))
        corr = (corr_low, corr_high)
    gradient, mine = call(
        gradient_kernel,
        [shear_modulus.shape, (DOT_ROWS, LANES)],
        [ints, *corr, shear_modulus, prior_mean, steps_taken, grad_change, static],
        cells * 20,
        "gradient",
        1,
    )
    (final,) = call(
        join_kernel, [field_now.shape], [ints, *now[0], *now[1]], cells, "join", 1
    )
    parts = sum_over_gz(mine)
    (direction,) = call(
        direction_kernel,
        [shear_modulus.shape],
        [parts, gradient, steps_taken, grad_change],
        cells * 20,
        "direction",
    )
    return (final, gradient, direction)


def solution(mesh):
    placed = (
        P("sample", "gz", None, None),
        P("sample", "gz", None, None),
        P("gz", "sample", None),
        P("gz", "sample", None),
        P("gz", "sample", None),
        P("sample", "gz", None, None),
        P("sample"),
        P("gz", "sample", None),
        P("sample", "gz", None, None),
        P("sample", "gz", None, None),
    )
    return jax.shard_map(
        on_device,
        mesh=mesh,
        in_specs=placed,
        out_specs=(P("sample", "gz", None, None), P("gz", "sample", None), P("gz", "sample", None)),
        check_vma=False,
    )
```

profile of v0, /device:TPU:0, one launch (start us, length us, event | category | flops | bytes accessed | tf_op | source)
XLA Modules:
  0.0 104.0 jit_solution(891605949832210359)
XLA Ops:
  3.3 3.0 %collective-permute-start = (f32[3,112,256]{2,1,0:T(8,128)S(1)}, f32[3,112,256]{2,1,0:T(8,128)S(1)}, u32[]{:S(2)}, u32[]{:S(2)}) collective-permute-start(f32[3,112,256]{2,1,0:T(8,128)S(1)} %get-tuple-element.64.refs_2_.refs_4_.refs_8_), channel_id=1, source_target_pairs={{1,2},{2,1},{3,4},{4,3},{5,6},{6,5},{0,8},{7,15},{9,10},{10,9},{11... | collective-permute-start | bytes 1032200 | tf_op jit(solution)/shard_map/ppermute | solution.py:418
  11.5 2.3 %step0_low.1 = (f32[3,104,256]{2,1,0:T(8,128)S(1)}, f32[3,104,256]{2,1,0:T(8,128)S(1)}, f32[2,104,256]{2,1,0:T(8,128)S(1)}) custom-call(s32[1]{0:T(128)} %bitcast.ip, f32[10]{0:T(128)S(1)} %pad_maximum_fusion.1.fs, f32[3,112,256]{2,1,0:T(8,128)S(1)} %collective-permute-done.refs_0_, f32[3,112,256]{2,1,0:T(8,128)S(1)} %collective-permute-done.1.refs_1_.refs_2_, ...), custom_call_target="tpu_custom_call" | custom-call | flops 6389760 | tf_op jit(solution)/shard_map/step0_low/pallas_call | solution.py:337
  13.8 2.1 %collective-permute-start.2 = (f32[3,104,256]{2,1,0:T(8,128)S(1)}, f32[3,104,256]{2,1,0:T(8,128)S(1)}, u32[]{:S(2)}, u32[]{:S(2)}) collective-permute-start(f32[3,104,256]{2,1,0:T(8,128)S(1)} %get-tuple-element.71.refs_2_.refs_4_.refs_8_), channel_id=1, source_target_pairs={{1,2},{2,1},{3,4},{4,3},{5,6},{6,5},{0,8},{7,15},{9,10},{10,9},{11... | collective-permute-start | bytes 958472 | tf_op jit(solution)/shard_map/ppermute | solution.py:418
  17.2 5.2 %collective-permute-done.16.refs_1_ = f32[3,48,256]{2,1,0:T(8,128)S(1)} collective-permute-done((f32[3,48,256]{2,1,0:T(8,128)S(1)}, f32[3,48,256]{2,1,0:T(8,128)S(1)}, u32[]{:S(2)}, u32[]{:S(2)}) %collective-permute-start.16) | collective-permute-done | bytes 147488 | tf_op jit(solution)/shard_map/ppermute | solution.py:418
  22.5 1.4 %step0_high.1 = (f32[3,56,256]{2,1,0:T(8,128)S(1)}, f32[3,56,256]{2,1,0:T(8,128)S(1)}, f32[2,56,256]{2,1,0:T(8,128)S(1)}) custom-call(s32[1]{0:T(128)} %bitcast.ip, f32[10]{0:T(128)S(1)} %pad_maximum_fusion.1.fs, f32[3,112,256]{2,1,0:T(8,128)S(1)} %collective-permute-done.refs_0_, f32[3,48,256]{2,1,0:T(8,128)S(1)} %collective-permute-done.16.refs_1_, ...), custom_call_target="tpu_custom_call" | custom-call | flops 3440640 | tf_op jit(solution)/shard_map/step0_high/pallas_call | solution.py:337
  23.9 2.1 %collective-permute-start.18 = (f32[3,56,256]{2,1,0:T(8,128)S(1)}, f32[3,56,256]{2,1,0:T(8,128)S(1)}, u32[]{:S(2)}, u32[]{:S(2)}) collective-permute-start(f32[3,56,256]{2,1,0:T(8,128)S(1)} %get-tuple-element.97.refs_5_.refs_9_), channel_id=1, source_target_pairs={{1,2},{2,1},{3,4},{4,3},{5,6},{6,5},{0,8},{7,15},{9,10},{10,9},{11... | collective-permute-start | bytes 516104 | tf_op jit(solution)/shard_map/ppermute | solution.py:418
  26.0 2.2 %step1_low.1 = (f32[3,96,256]{2,1,0:T(8,128)S(1)}, f32[3,96,256]{2,1,0:T(8,128)S(1)}, f32[2,96,256]{2,1,0:T(8,128)S(1)}) custom-call(s32[1]{0:T(128)} %bitcast.ip, f32[10]{0:T(128)S(1)} %pad_maximum_fusion.1.fs, f32[3,104,256]{2,1,0:T(8,128)S(1)} %collective-permute-done.2.refs_0_, f32[3,104,256]{2,1,0:T(8,128)S(1)} %collective-permute-done.3.refs_1_.refs_2_, ...), custom_call_target="tpu_custom_call" | custom-call | flops 5898240 | tf_op jit(solution)/shard_map/step1_low/pallas_call | solution.py:337
  29.3 1.6 %step1_high.1 = (f32[3,64,256]{2,1,0:T(8,128)S(1)}, f32[3,64,256]{2,1,0:T(8,128)S(1)}, f32[2,64,256]{2,1,0:T(8,128)S(1)}) custom-call(s32[1]{0:T(128)} %bitcast.ip, f32[10]{0:T(128)S(1)} %pad_maximum_fusion.1.fs, f32[3,104,256]{2,1,0:T(8,128)S(1)} %collective-permute-done.2.refs_0_, f32[3,56,256]{2,1,0:T(8,128)S(1)} %collective-permute-done.18.refs_1_, ...), custom_call_target="tpu_custom_call" | custom-call | flops 3932160 | tf_op jit(solution)/shard_map/step1_high/pallas_call | solution.py:337
  30.9 2.1 %collective-permute-start.20 = (f32[3,64,256]{2,1,0:T(8,128)S(1)}, f32[3,64,256]{2,1,0:T(8,128)S(1)}, u32[]{:S(2)}, u32[]{:S(2)}) collective-permute-start(f32[3,64,256]{2,1,0:T(8,128)S(1)} %get-tuple-element.100.refs_5_.refs_9_), channel_id=1, source_target_pairs={{1,2},{2,1},{3,4},{4,3},{5,6},{6,5},{0,8},{7,15},{9,10},{10,9},{11... | collective-permute-start | bytes 589832 | tf_op jit(solution)/shard_map/ppermute | solution.py:418
  33.0 1.9 %collective-permute-done.4.refs_0_ = f32[3,96,256]{2,1,0:T(8,128)S(1)} collective-permute-done((f32[3,96,256]{2,1,0:T(8,128)S(1)}, f32[3,96,256]{2,1,0:T(8,128)S(1)}, u32[]{:S(2)}, u32[]{:S(2)}) %collective-permute-start.4) | collective-permute-done | bytes 294944 | tf_op jit(solution)/shard_map/ppermute | solution.py:418
  34.9 2.0 %step2_low.1 = (f32[3,88,256]{2,1,0:T(8,128)S(1)}, f32[3,88,256]{2,1,0:T(8,128)S(1)}, f32[2,88,256]{2,1,0:T(8,128)S(1)}) custom-call(s32[1]{0:T(128)} %bitcast.ip, f32[10]{0:T(128)S(1)} %pad_maximum_fusion.1.fs, f32[3,96,256]{2,1,0:T(8,128)S(1)} %collective-permute-done.4.refs_0_, f32[3,96,256]{2,1,0:T(8,128)S(1)} %collective-permute-done.5.refs_1_.refs_2_, ...), custom_call_target="tpu_custom_call" | custom-call | flops 5406720 | tf_op jit(solution)/shard_map/step2_low/pallas_call | solution.py:337
  37.6 1.7 %step2_high.1 = (f32[3,72,256]{2,1,0:T(8,128)S(1)}, f32[3,72,256]{2,1,0:T(8,128)S(1)}, f32[2,72,256]{2,1,0:T(8,128)S(1)}) custom-call(s32[1]{0:T(128)} %bitcast.ip, f32[10]{0:T(128)S(1)} %pad_maximum_fusion.1.fs, f32[3,96,256]{2,1,0:T(8,128)S(1)} %collective-permute-done.4.refs_0_, f32[3,64,256]{2,1,0:T(8,128)S(1)} %collective-permute-done.20.refs_1_, ...), custom_call_target="tpu_custom_call" | custom-call | flops 4423680 | tf_op jit(solution)/shard_map/step2_high/pallas_call | solution.py:337
  39.3 1.6 %collective-permute-start.22 = (f32[3,72,256]{2,1,0:T(8,128)S(1)}, f32[3,72,256]{2,1,0:T(8,128)S(1)}, u32[]{:S(2)}, u32[]{:S(2)}) collective-permute-start(f32[3,72,256]{2,1,0:T(8,128)S(1)} %get-tuple-element.103.refs_5_.refs_9_), channel_id=1, source_target_pairs={{1,2},{2,1},{3,4},{4,3},{5,6},{6,5},{0,8},{7,15},{9,10},{10,9},{11... | collective-permute-start | bytes 663560 | tf_op jit(solution)/shard_map/ppermute | solution.py:418
  40.9 5.0 %collective-permute-done.22.refs_1_ = f32[3,72,256]{2,1,0:T(8,128)S(1)} collective-permute-done((f32[3,72,256]{2,1,0:T(8,128)S(1)}, f32[3,72,256]{2,1,0:T(8,128)S(1)}, u32[]{:S(2)}, u32[]{:S(2)}) %collective-permute-start.22) | collective-permute-done | bytes 221216 | tf_op jit(solution)/shard_map/ppermute | solution.py:418
  45.9 1.8 %step3_high.1 = (f32[3,80,256]{2,1,0:T(8,128)S(1)}, f32[3,80,256]{2,1,0:T(8,128)S(1)}, f32[2,80,256]{2,1,0:T(8,128)S(1)}) custom-call(s32[1]{0:T(128)} %bitcast.ip, f32[10]{0:T(128)S(1)} %pad_maximum_fusion.1.fs, f32[3,88,256]{2,1,0:T(8,128)S(1)} %collective-permute-done.6.refs_0_, f32[3,72,256]{2,1,0:T(8,128)S(1)} %collective-permute-done.22.refs_1_, ...), custom_call_target="tpu_custom_call" | custom-call | flops 4915200 | tf_op jit(solution)/shard_map/step3_high/pallas_call | solution.py:337
  48.7 1.9 %step3_low.1 = (f32[3,80,256]{2,1,0:T(8,128)S(1)}, f32[3,80,256]{2,1,0:T(8,128)S(1)}, f32[2,80,256]{2,1,0:T(8,128)S(1)}) custom-call(s32[1]{0:T(128)} %bitcast.ip, f32[10]{0:T(128)S(1)} %pad_maximum_fusion.1.fs, f32[3,88,256]{2,1,0:T(8,128)S(1)} %collective-permute-done.6.refs_0_, f32[3,88,256]{2,1,0:T(8,128)S(1)} %collective-permute-done.7.refs_1_.refs_2_, ...), custom_call_target="tpu_custom_call" | custom-call | flops 4915200 | tf_op jit(solution)/shard_map/step3_low/pallas_call | solution.py:337
  51.8 2.2 %collective-permute-done.24.refs_1_ = f32[3,80,256]{2,1,0:T(8,128)S(1)} collective-permute-done((f32[3,80,256]{2,1,0:T(8,128)S(1)}, f32[3,80,256]{2,1,0:T(8,128)S(1)}, u32[]{:S(2)}, u32[]{:S(2)}) %collective-permute-start.24) | collective-permute-done | bytes 245792 | tf_op jit(solution)/shard_map/ppermute | solution.py:418
  54.0 2.9 %collective-permute-done.8.refs_0_ = f32[3,80,256]{2,1,0:T(8,128)S(1)} collective-permute-done((f32[3,80,256]{2,1,0:T(8,128)S(1)}, f32[3,80,256]{2,1,0:T(8,128)S(1)}, u32[]{:S(2)}, u32[]{:S(2)}) %collective-permute-start.8) | collective-permute-done | bytes 245792 | tf_op jit(solution)/shard_map/ppermute | solution.py:418
  56.9 1.9 %step4_high.1 = (f32[3,88,256]{2,1,0:T(8,128)S(1)}, f32[3,88,256]{2,1,0:T(8,128)S(1)}, f32[2,88,256]{2,1,0:T(8,128)S(1)}) custom-call(s32[1]{0:T(128)} %bitcast.ip, f32[10]{0:T(128)S(1)} %pad_maximum_fusion.1.fs, f32[3,80,256]{2,1,0:T(8,128)S(1)} %collective-permute-done.8.refs_0_, f32[3,80,256]{2,1,0:T(8,128)S(1)} %collective-permute-done.24.refs_1_, ...), custom_call_target="tpu_custom_call" | custom-call | flops 5406720 | tf_op jit(solution)/shard_map/step4_high/pallas_call | solution.py:337
  60.0 1.8 %step4_low.1 = (f32[3,72,256]{2,1,0:T(8,128)S(1)}, f32[3,72,256]{2,1,0:T(8,128)S(1)}, f32[2,72,256]{2,1,0:T(8,128)S(1)}) custom-call(s32[1]{0:T(128)} %bitcast.ip, f32[10]{0:T(128)S(1)} %pad_maximum_fusion.1.fs, f32[3,80,256]{2,1,0:T(8,128)S(1)} %collective-permute-done.8.refs_0_, f32[3,80,256]{2,1,0:T(8,128)S(1)} %collective-permute-done.9.refs_1_.refs_2_, ...), custom_call_target="tpu_custom_call" | custom-call | flops 4423680 | tf_op jit(solution)/shard_map/step4_low/pallas_call | solution.py:337
  62.8 5.0 %collective-permute-done.10.refs_0_ = f32[3,72,256]{2,1,0:T(8,128)S(1)} collective-permute-done((f32[3,72,256]{2,1,0:T(8,128)S(1)}, f32[3,72,256]{2,1,0:T(8,128)S(1)}, u32[]{:S(2)}, u32[]{:S(2)}) %collective-permute-start.10) | collective-permute-done | bytes 221216 | tf_op jit(solution)/shard_map/ppermute | solution.py:418
  67.8 2.1 %step5_high.1 = (f32[3,96,256]{2,1,0:T(8,128)S(1)}, f32[3,96,256]{2,1,0:T(8,128)S(1)}, f32[2,96,256]{2,1,0:T(8,128)S(1)}) custom-call(s32[1]{0:T(128)} %bitcast.ip, f32[10]{0:T(128)S(1)} %pad_maximum_fusion.1.fs, f32[3,72,256]{2,1,0:T(8,128)S(1)} %collective-permute-done.10.refs_0_, f32[3,88,256]{2,1,0:T(8,128)S(1)} %collective-permute-done.26.refs_1_, ...), custom_call_target="tpu_custom_call" | custom-call | flops 5898240 | tf_op jit(solution)/shard_map/step5_high/pallas_call | solution.py:337
  71.1 1.6 %step5_low.1 = (f32[3,64,256]{2,1,0:T(8,128)S(1)}, f32[3,64,256]{2,1,0:T(8,128)S(1)}, f32[2,64,256]{2,1,0:T(8,128)S(1)}) custom-call(s32[1]{0:T(128)} %bitcast.ip, f32[10]{0:T(128)S(1)} %pad_maximum_fusion.1.fs, f32[3,72,256]{2,1,0:T(8,128)S(1)} %collective-permute-done.10.refs_0_, f32[3,72,256]{2,1,0:T(8,128)S(1)} %collective-permute-done.11.refs_1_.refs_2_, ...), custom_call_target="tpu_custom_call" | custom-call | flops 3932160 | tf_op jit(solution)/shard_map/step5_low/pallas_call | solution.py:337
  73.7 5.1 %collective-permute-done.12.refs_0_ = f32[3,64,256]{2,1,0:T(8,128)S(1)} collective-permute-done((f32[3,64,256]{2,1,0:T(8,128)S(1)}, f32[3,64,256]{2,1,0:T(8,128)S(1)}, u32[]{:S(2)}, u32[]{:S(2)}) %collective-permute-start.12) | collective-permute-done | bytes 196640 | tf_op jit(solution)/shard_map/ppermute | solution.py:418
  78.8 2.2 %step6_high.1 = (f32[3,104,256]{2,1,0:T(8,128)S(1)}, f32[3,104,256]{2,1,0:T(8,128)S(1)}, f32[2,104,256]{2,1,0:T(8,128)S(1)}) custom-call(s32[1]{0:T(128)} %bitcast.ip, f32[10]{0:T(128)S(1)} %pad_maximum_fusion.1.fs, f32[3,64,256]{2,1,0:T(8,128)S(1)} %collective-permute-done.12.refs_0_, f32[3,96,256]{2,1,0:T(8,128)S(1)} %collective-permute-done.28.refs_1_, ...), custom_call_target="tpu_custom_call" | custom-call | flops 6389760 | tf_op jit(solution)/shard_map/step6_high/pallas_call | solution.py:337
  82.2 1.5 %step6_low.1 = (f32[3,56,256]{2,1,0:T(8,128)S(1)}, f32[3,56,256]{2,1,0:T(8,128)S(1)}, f32[2,56,256]{2,1,0:T(8,128)S(1)}) custom-call(s32[1]{0:T(128)} %bitcast.ip, f32[10]{0:T(128)S(1)} %pad_maximum_fusion.1.fs, f32[3,64,256]{2,1,0:T(8,128)S(1)} %collective-permute-done.12.refs_0_, f32[3,64,256]{2,1,0:T(8,128)S(1)} %collective-permute-done.13.refs_1_.refs_2_, ...), custom_call_target="tpu_custom_call" | custom-call | flops 3440640 | tf_op jit(solution)/shard_map/step6_low/pallas_call | solution.py:337
  85.4 4.6 %collective-permute-done.14.refs_0_ = f32[3,56,256]{2,1,0:T(8,128)S(1)} collective-permute-done((f32[3,56,256]{2,1,0:T(8,128)S(1)}, f32[3,56,256]{2,1,0:T(8,128)S(1)}, u32[]{:S(2)}, u32[]{:S(2)}) %collective-permute-start.14) | collective-permute-done | bytes 172064 | tf_op jit(solution)/shard_map/ppermute | solution.py:418
  90.0 1.4 %step7_low.1 = (f32[3,48,256]{2,1,0:T(8,128)S(1)}, f32[3,48,256]{2,1,0:T(8,128)S(1)}, f32[2,48,256]{2,1,0:T(8,128)S(1)}) custom-call(s32[1]{0:T(128)} %bitcast.ip, f32[10]{0:T(128)S(1)} %pad_maximum_fusion.1.fs, f32[3,56,256]{2,1,0:T(8,128)S(1)} %collective-permute-done.14.refs_0_, f32[3,56,256]{2,1,0:T(8,128)S(1)} %collective-permute-done.15.refs_1_.refs_2_, ...), custom_call_target="tpu_custom_call" | custom-call | flops 2949120 | tf_op jit(solution)/shard_map/step7_low/pallas_call | solution.py:337
  91.4 2.4 %step7_high.1 = (f32[3,112,256]{2,1,0:T(8,128)S(1)}, f32[3,112,256]{2,1,0:T(8,128)S(1)}, f32[2,112,256]{2,1,0:T(8,128)S(1)}) custom-call(s32[1]{0:T(128)} %bitcast.ip, f32[10]{0:T(128)S(1)} %pad_maximum_fusion.1.fs, f32[3,56,256]{2,1,0:T(8,128)S(1)} %collective-permute-done.14.refs_0_, f32[3,104,256]{2,1,0:T(8,128)S(1)} %collective-permute-done.30.refs_1_, ...), custom_call_target="tpu_custom_call" | custom-call | flops 6881280 | tf_op jit(solution)/shard_map/step7_high/pallas_call | solution.py:337
  96.9 1.3 %collective-permute-start.33 = (f32[32,128]{1,0:T(8,128)S(1)}, f32[32,128]{1,0:T(8,128)S(1)}, u32[]{:S(2)}, u32[]{:S(2)}) collective-permute-start(f32[32,128]{1,0:T(8,128)S(1)} %add.8), channel_id=1, source_target_pairs={{0,2},{1,3},{2,4},{3,5},{4,6},{5,7},{6,0},{7,1},{8,10},{9,11},{10,... | collective-permute-start | bytes 49160 | tf_op jit(solution)/shard_map/ppermute | solution.py:369
  100.8 1.6 %collective-permute-done.33 = f32[32,128]{1,0:T(8,128)S(1)} collective-permute-done((f32[32,128]{1,0:T(8,128)S(1)}, f32[32,128]{1,0:T(8,128)S(1)}, u32[]{:S(2)}, u32[]{:S(2)}) %collective-permute-start.33) | collective-permute-done | bytes 16416 | tf_op jit(solution)/shard_map/ppermute | solution.py:369
  102.4 1.6 %direction.1 = f32[2,160,256]{2,1,0:T(8,128)} custom-call(f32[4,32,128]{2,1,0:T(8,128)S(1)} %pad_maximum_fusion.parts, f32[2,160,256]{2,1,0:T(8,128)S(1)} %copy-done.10, f32[4,2,160,256]{3,2,1,0:T(8,128)S(1)} %copy-done.1, f32[4,2,160,256]{3,2,1,0:T(8,128)S(1)} %copy-done.2), custom_call_target="tpu_custom_call" | custom-call | flops 1638400 | tf_op jit(solution)/shard_map/direction/pallas_call | solution.py:337
  (100 shorter events, 26.0 us)
Async XLA Ops:
  3.3 8.2 %collective-permute-start = (f32[3,112,256]{2,1,0:T(8,128)S(1)}, f32[3,112,256]{2,1,0:T(8,128)S(1)}, u32[]{:S(2)}, u32[]{:S(2)}) collective-permute-start(f32[3,112,256]{2,1,0:T(8,128)S(1)} %get-tuple-element.64.refs_2_.refs_4_.refs_8_), channel_id=1, source_target_pairs={{1,2},{2,1},{3,4},{4,3},{5,6},{6,5},{0,8},{7,15},{9,10},{10,9},{11... | collective-permute-start | bytes 1032200 | tf_op jit(solution)/shard_map/ppermute | solution.py:418
  6.3 5.2 %collective-permute-start.1 = (f32[3,112,256]{2,1,0:T(8,128)S(1)}, f32[3,112,256]{2,1,0:T(8,128)S(1)}, u32[]{:S(2)}, u32[]{:S(2)}) collective-permute-start(f32[3,112,256]{2,1,0:T(8,128)S(1)} %get-tuple-element.65.refs_3_.refs_5_.refs_6_.refs_10_), channel_id=1, source_target_pairs={{0,1},{1,0},{2,3},{3,2},{4,5},{5,4},{6,7},{7,6},{8,9},{9,8},{10,11... | collective-permute-start | bytes 1032200 | tf_op jit(solution)/shard_map/ppermute | solution.py:419
  13.8 12.1 %collective-permute-start.2 = (f32[3,104,256]{2,1,0:T(8,128)S(1)}, f32[3,104,256]{2,1,0:T(8,128)S(1)}, u32[]{:S(2)}, u32[]{:S(2)}) collective-permute-start(f32[3,104,256]{2,1,0:T(8,128)S(1)} %get-tuple-element.71.refs_2_.refs_4_.refs_8_), channel_id=1, source_target_pairs={{1,2},{2,1},{3,4},{4,3},{5,6},{6,5},{0,8},{7,15},{9,10},{10,9},{11... | collective-permute-start | bytes 958472 | tf_op jit(solution)/shard_map/ppermute | solution.py:418
  15.9 10.1 %collective-permute-start.3 = (f32[3,104,256]{2,1,0:T(8,128)S(1)}, f32[3,104,256]{2,1,0:T(8,128)S(1)}, u32[]{:S(2)}, u32[]{:S(2)}) collective-permute-start(f32[3,104,256]{2,1,0:T(8,128)S(1)} %get-tuple-element.72.refs_3_.refs_5_.refs_6_.refs_10_), channel_id=1, source_target_pairs={{0,1},{1,0},{2,3},{3,2},{4,5},{5,4},{6,7},{7,6},{8,9},{9,8},{10,11... | collective-permute-start | bytes 958472 | tf_op jit(solution)/shard_map/ppermute | solution.py:419
  15.9 6.5 %collective-permute-start.16 = (f32[3,48,256]{2,1,0:T(8,128)S(1)}, f32[3,48,256]{2,1,0:T(8,128)S(1)}, u32[]{:S(2)}, u32[]{:S(2)}) collective-permute-start(f32[3,48,256]{2,1,0:T(8,128)S(1)} %copy-done.7), channel_id=1, source_target_pairs={{1,2},{2,1},{3,4},{4,3},{5,6},{6,5},{0,8},{7,15},{9,10},{10,9},{11... | collective-permute-start | bytes 442376 | tf_op jit(solution)/shard_map/ppermute | solution.py:418
  17.0 5.4 %collective-permute-start.17 = (f32[3,48,256]{2,1,0:T(8,128)S(1)}, f32[3,48,256]{2,1,0:T(8,128)S(1)}, u32[]{:S(2)}, u32[]{:S(2)}) collective-permute-start(f32[3,48,256]{2,1,0:T(8,128)S(1)} %copy-done.9), channel_id=1, source_target_pairs={{0,1},{1,0},{2,3},{3,2},{4,5},{5,4},{6,7},{7,6},{8,9},{9,8},{10,11... | collective-permute-start | bytes 442376 | tf_op jit(solution)/shard_map/ppermute | solution.py:419
  23.9 5.5 %collective-permute-start.18 = (f32[3,56,256]{2,1,0:T(8,128)S(1)}, f32[3,56,256]{2,1,0:T(8,128)S(1)}, u32[]{:S(2)}, u32[]{:S(2)}) collective-permute-start(f32[3,56,256]{2,1,0:T(8,128)S(1)} %get-tuple-element.97.refs_5_.refs_9_), channel_id=1, source_target_pairs={{1,2},{2,1},{3,4},{4,3},{5,6},{6,5},{0,8},{7,15},{9,10},{10,9},{11... | collective-permute-start | bytes 516104 | tf_op jit(solution)/shard_map/ppermute | solution.py:418
  28.1 6.8 %collective-permute-start.4 = (f32[3,96,256]{2,1,0:T(8,128)S(1)}, f32[3,96,256]{2,1,0:T(8,128)S(1)}, u32[]{:S(2)}, u32[]{:S(2)}) collective-permute-start(f32[3,96,256]{2,1,0:T(8,128)S(1)} %get-tuple-element.74.refs_2_.refs_4_.refs_8_), channel_id=1, source_target_pairs={{1,2},{2,1},{3,4},{4,3},{5,6},{6,5},{0,8},{7,15},{9,10},{10,9},{11... | collective-permute-start | bytes 884744 | tf_op jit(solution)/shard_map/ppermute | solution.py:418
  28.7 6.2 %collective-permute-start.5 = (f32[3,96,256]{2,1,0:T(8,128)S(1)}, f32[3,96,256]{2,1,0:T(8,128)S(1)}, u32[]{:S(2)}, u32[]{:S(2)}) collective-permute-start(f32[3,96,256]{2,1,0:T(8,128)S(1)} %get-tuple-element.75.refs_3_.refs_5_.refs_6_.refs_10_), channel_id=1, source_target_pairs={{0,1},{1,0},{2,3},{3,2},{4,5},{5,4},{6,7},{7,6},{8,9},{9,8},{10,11... | collective-permute-start | bytes 884744 | tf_op jit(solution)/shard_map/ppermute | solution.py:419
  30.9 6.7 %collective-permute-start.20 = (f32[3,64,256]{2,1,0:T(8,128)S(1)}, f32[3,64,256]{2,1,0:T(8,128)S(1)}, u32[]{:S(2)}, u32[]{:S(2)}) collective-permute-start(f32[3,64,256]{2,1,0:T(8,128)S(1)} %get-tuple-element.100.refs_5_.refs_9_), channel_id=1, source_target_pairs={{1,2},{2,1},{3,4},{4,3},{5,6},{6,5},{0,8},{7,15},{9,10},{10,9},{11... | collective-permute-start | bytes 589832 | tf_op jit(solution)/shard_map/ppermute | solution.py:418
  37.0 8.9 %collective-permute-start.6 = (f32[3,88,256]{2,1,0:T(8,128)S(1)}, f32[3,88,256]{2,1,0:T(8,128)S(1)}, u32[]{:S(2)}, u32[]{:S(2)}) collective-permute-start(f32[3,88,256]{2,1,0:T(8,128)S(1)} %get-tuple-element.77.refs_2_.refs_4_.refs_8_), channel_id=1, source_target_pairs={{1,2},{2,1},{3,4},{4,3},{5,6},{6,5},{0,8},{7,15},{9,10},{10,9},{11... | collective-permute-start | bytes 811016 | tf_op jit(solution)/shard_map/ppermute | solution.py:418
  37.6 8.3 %collective-permute-start.7 = (f32[3,88,256]{2,1,0:T(8,128)S(1)}, f32[3,88,256]{2,1,0:T(8,128)S(1)}, u32[]{:S(2)}, u32[]{:S(2)}) collective-permute-start(f32[3,88,256]{2,1,0:T(8,128)S(1)} %get-tuple-element.78.refs_3_.refs_5_.refs_6_.refs_10_), channel_id=1, source_target_pairs={{0,1},{1,0},{2,3},{3,2},{4,5},{5,4},{6,7},{7,6},{8,9},{9,8},{10,11... | collective-permute-start | bytes 811016 | tf_op jit(solution)/shard_map/ppermute | solution.py:419
  39.3 6.6 %collective-permute-start.22 = (f32[3,72,256]{2,1,0:T(8,128)S(1)}, f32[3,72,256]{2,1,0:T(8,128)S(1)}, u32[]{:S(2)}, u32[]{:S(2)}) collective-permute-start(f32[3,72,256]{2,1,0:T(8,128)S(1)} %get-tuple-element.103.refs_5_.refs_9_), channel_id=1, source_target_pairs={{1,2},{2,1},{3,4},{4,3},{5,6},{6,5},{0,8},{7,15},{9,10},{10,9},{11... | collective-permute-start | bytes 663560 | tf_op jit(solution)/shard_map/ppermute | solution.py:418
  40.9 5.0 %collective-permute-start.23 = (f32[3,72,256]{2,1,0:T(8,128)S(1)}, f32[3,72,256]{2,1,0:T(8,128)S(1)}, u32[]{:S(2)}, u32[]{:S(2)}) collective-permute-start(f32[3,72,256]{2,1,0:T(8,128)S(1)} %get-tuple-element.104.refs_7_.refs_11_), channel_id=1, source_target_pairs={{0,1},{1,0},{2,3},{3,2},{4,5},{5,4},{6,7},{7,6},{8,9},{9,8},{10,11... | collective-permute-start | bytes 663560 | tf_op jit(solution)/shard_map/ppermute | solution.py:419
  47.7 6.3 %collective-permute-start.24 = (f32[3,80,256]{2,1,0:T(8,128)S(1)}, f32[3,80,256]{2,1,0:T(8,128)S(1)}, u32[]{:S(2)}, u32[]{:S(2)}) collective-permute-start(f32[3,80,256]{2,1,0:T(8,128)S(1)} %get-tuple-element.106.refs_5_.refs_9_), channel_id=1, source_target_pairs={{1,2},{2,1},{3,4},{4,3},{5,6},{6,5},{0,8},{7,15},{9,10},{10,9},{11... | collective-permute-start | bytes 737288 | tf_op jit(solution)/shard_map/ppermute | solution.py:418
  48.7 5.3 %collective-permute-start.25 = (f32[3,80,256]{2,1,0:T(8,128)S(1)}, f32[3,80,256]{2,1,0:T(8,128)S(1)}, u32[]{:S(2)}, u32[]{:S(2)}) collective-permute-start(f32[3,80,256]{2,1,0:T(8,128)S(1)} %get-tuple-element.107.refs_7_.refs_11_), channel_id=1, source_target_pairs={{0,1},{1,0},{2,3},{3,2},{4,5},{5,4},{6,7},{7,6},{8,9},{9,8},{10,11... | collective-permute-start | bytes 737288 | tf_op jit(solution)/shard_map/ppermute | solution.py:419
  50.6 6.3 %collective-permute-start.8 = (f32[3,80,256]{2,1,0:T(8,128)S(1)}, f32[3,80,256]{2,1,0:T(8,128)S(1)}, u32[]{:S(2)}, u32[]{:S(2)}) collective-permute-start(f32[3,80,256]{2,1,0:T(8,128)S(1)} %get-tuple-element.80.refs_2_.refs_4_.refs_8_), channel_id=1, source_target_pairs={{1,2},{2,1},{3,4},{4,3},{5,6},{6,5},{0,8},{7,15},{9,10},{10,9},{11... | collective-permute-start | bytes 737288 | tf_op jit(solution)/shard_map/ppermute | solution.py:418
  51.8 5.1 %collective-permute-start.9 = (f32[3,80,256]{2,1,0:T(8,128)S(1)}, f32[3,80,256]{2,1,0:T(8,128)S(1)}, u32[]{:S(2)}, u32[]{:S(2)}) collective-permute-start(f32[3,80,256]{2,1,0:T(8,128)S(1)} %get-tuple-element.81.refs_3_.refs_5_.refs_6_.refs_10_), channel_id=1, source_target_pairs={{0,1},{1,0},{2,3},{3,2},{4,5},{5,4},{6,7},{7,6},{8,9},{9,8},{10,11... | collective-permute-start | bytes 737288 | tf_op jit(solution)/shard_map/ppermute | solution.py:419
  58.9 8.9 %collective-permute-start.26 = (f32[3,88,256]{2,1,0:T(8,128)S(1)}, f32[3,88,256]{2,1,0:T(8,128)S(1)}, u32[]{:S(2)}, u32[]{:S(2)}) collective-permute-start(f32[3,88,256]{2,1,0:T(8,128)S(1)} %get-tuple-element.109.refs_5_.refs_9_), channel_id=1, source_target_pairs={{1,2},{2,1},{3,4},{4,3},{5,6},{6,5},{0,8},{7,15},{9,10},{10,9},{11... | collective-permute-start | bytes 811016 | tf_op jit(solution)/shard_map/ppermute | solution.py:418
  60.0 7.8 %collective-permute-start.27 = (f32[3,88,256]{2,1,0:T(8,128)S(1)}, f32[3,88,256]{2,1,0:T(8,128)S(1)}, u32[]{:S(2)}, u32[]{:S(2)}) collective-permute-start(f32[3,88,256]{2,1,0:T(8,128)S(1)} %get-tuple-element.110.refs_7_.refs_11_), channel_id=1, source_target_pairs={{0,1},{1,0},{2,3},{3,2},{4,5},{5,4},{6,7},{7,6},{8,9},{9,8},{10,11... | collective-permute-start | bytes 811016 | tf_op jit(solution)/shard_map/ppermute | solution.py:419
  61.8 6.0 %collective-permute-start.10 = (f32[3,72,256]{2,1,0:T(8,128)S(1)}, f32[3,72,256]{2,1,0:T(8,128)S(1)}, u32[]{:S(2)}, u32[]{:S(2)}) collective-permute-start(f32[3,72,256]{2,1,0:T(8,128)S(1)} %get-tuple-element.83.refs_2_.refs_4_.refs_8_), channel_id=1, source_target_pairs={{1,2},{2,1},{3,4},{4,3},{5,6},{6,5},{0,8},{7,15},{9,10},{10,9},{11... | collective-permute-start | bytes 663560 | tf_op jit(solution)/shard_map/ppermute | solution.py:418
  62.8 5.0 %collective-permute-start.11 = (f32[3,72,256]{2,1,0:T(8,128)S(1)}, f32[3,72,256]{2,1,0:T(8,128)S(1)}, u32[]{:S(2)}, u32[]{:S(2)}) collective-permute-start(f32[3,72,256]{2,1,0:T(8,128)S(1)} %get-tuple-element.84.refs_3_.refs_5_.refs_6_.refs_10_), channel_id=1, source_target_pairs={{0,1},{1,0},{2,3},{3,2},{4,5},{5,4},{6,7},{7,6},{8,9},{9,8},{10,11... | collective-permute-start | bytes 663560 | tf_op jit(solution)/shard_map/ppermute | solution.py:419
  69.9 8.9 %collective-permute-start.28 = (f32[3,96,256]{2,1,0:T(8,128)S(1)}, f32[3,96,256]{2,1,0:T(8,128)S(1)}, u32[]{:S(2)}, u32[]{:S(2)}) collective-permute-start(f32[3,96,256]{2,1,0:T(8,128)S(1)} %get-tuple-element.112.refs_5_.refs_9_), channel_id=1, source_target_pairs={{1,2},{2,1},{3,4},{4,3},{5,6},{6,5},{0,8},{7,15},{9,10},{10,9},{11... | collective-permute-start | bytes 884744 | tf_op jit(solution)/shard_map/ppermute | solution.py:418
  71.1 7.8 %collective-permute-start.29 = (f32[3,96,256]{2,1,0:T(8,128)S(1)}, f32[3,96,256]{2,1,0:T(8,128)S(1)}, u32[]{:S(2)}, u32[]{:S(2)}) collective-permute-start(f32[3,96,256]{2,1,0:T(8,128)S(1)} %get-tuple-element.113.refs_7_.refs_11_), channel_id=1, source_target_pairs={{0,1},{1,0},{2,3},{3,2},{4,5},{5,4},{6,7},{7,6},{8,9},{9,8},{10,11... | collective-permute-start | bytes 884744 | tf_op jit(solution)/shard_map/ppermute | solution.py:419
  72.7 6.1 %collective-permute-start.12 = (f32[3,64,256]{2,1,0:T(8,128)S(1)}, f32[3,64,256]{2,1,0:T(8,128)S(1)}, u32[]{:S(2)}, u32[]{:S(2)}) collective-permute-start(f32[3,64,256]{2,1,0:T(8,128)S(1)} %get-tuple-element.86.refs_2_.refs_4_.refs_8_), channel_id=1, source_target_pairs={{1,2},{2,1},{3,4},{4,3},{5,6},{6,5},{0,8},{7,15},{9,10},{10,9},{11... | collective-permute-start | bytes 589832 | tf_op jit(solution)/shard_map/ppermute | solution.py:418
  73.7 5.1 %collective-permute-start.13 = (f32[3,64,256]{2,1,0:T(8,128)S(1)}, f32[3,64,256]{2,1,0:T(8,128)S(1)}, u32[]{:S(2)}, u32[]{:S(2)}) collective-permute-start(f32[3,64,256]{2,1,0:T(8,128)S(1)} %get-tuple-element.87.refs_3_.refs_5_.refs_6_.refs_10_), channel_id=1, source_target_pairs={{0,1},{1,0},{2,3},{3,2},{4,5},{5,4},{6,7},{7,6},{8,9},{9,8},{10,11... | collective-permute-start | bytes 589832 | tf_op jit(solution)/shard_map/ppermute | solution.py:419
  81.1 10.3 %collective-permute-start.30 = (f32[3,104,256]{2,1,0:T(8,128)S(1)}, f32[3,104,256]{2,1,0:T(8,128)S(1)}, u32[]{:S(2)}, u32[]{:S(2)}) collective-permute-start(f32[3,104,256]{2,1,0:T(8,128)S(1)} %get-tuple-element.115.refs_5_), channel_id=1, source_target_pairs={{1,2},{2,1},{3,4},{4,3},{5,6},{6,5},{0,8},{7,15},{9,10},{10,9},{11... | collective-permute-start | bytes 958472 | tf_op jit(solution)/shard_map/ppermute | solution.py:418
  82.2 9.1 %collective-permute-start.31 = (f32[3,104,256]{2,1,0:T(8,128)S(1)}, f32[3,104,256]{2,1,0:T(8,128)S(1)}, u32[]{:S(2)}, u32[]{:S(2)}) collective-permute-start(f32[3,104,256]{2,1,0:T(8,128)S(1)} %get-tuple-element.116.refs_7_), channel_id=1, source_target_pairs={{0,1},{1,0},{2,3},{3,2},{4,5},{5,4},{6,7},{7,6},{8,9},{9,8},{10,11... | collective-permute-start | bytes 958472 | tf_op jit(solution)/shard_map/ppermute | solution.py:419
  83.7 6.3 %collective-permute-start.14 = (f32[3,56,256]{2,1,0:T(8,128)S(1)}, f32[3,56,256]{2,1,0:T(8,128)S(1)}, u32[]{:S(2)}, u32[]{:S(2)}) collective-permute-start(f32[3,56,256]{2,1,0:T(8,128)S(1)} %get-tuple-element.89.refs_2_.refs_4_), channel_id=1, source_target_pairs={{1,2},{2,1},{3,4},{4,3},{5,6},{6,5},{0,8},{7,15},{9,10},{10,9},{11... | collective-permute-start | bytes 516104 | tf_op jit(solution)/shard_map/ppermute | solution.py:418
  84.8 5.2 %collective-permute-start.15 = (f32[3,56,256]{2,1,0:T(8,128)S(1)}, f32[3,56,256]{2,1,0:T(8,128)S(1)}, u32[]{:S(2)}, u32[]{:S(2)}) collective-permute-start(f32[3,56,256]{2,1,0:T(8,128)S(1)} %get-tuple-element.90.refs_3_.refs_6_), channel_id=1, source_target_pairs={{0,1},{1,0},{2,3},{3,2},{4,5},{5,4},{6,7},{7,6},{8,9},{9,8},{10,11... | collective-permute-start | bytes 516104 | tf_op jit(solution)/shard_map/ppermute | solution.py:419
  96.1 4.7 %collective-permute-start.34 = (f32[32,128]{1,0:T(8,128)S(1)}, f32[32,128]{1,0:T(8,128)S(1)}, u32[]{:S(2)}, u32[]{:S(2)}) collective-permute-start(f32[32,128]{1,0:T(8,128)S(1)} %add.8), channel_id=1, source_target_pairs={{0,4},{1,5},{2,6},{3,7},{4,0},{5,1},{6,2},{7,3},{8,12},{9,13},{10,... | collective-permute-start | bytes 49160 | tf_op jit(solution)/shard_map/ppermute | solution.py:369
  96.9 5.5 %collective-permute-start.33 = (f32[32,128]{1,0:T(8,128)S(1)}, f32[32,128]{1,0:T(8,128)S(1)}, u32[]{:S(2)}, u32[]{:S(2)}) collective-permute-start(f32[32,128]{1,0:T(8,128)S(1)} %add.8), channel_id=1, source_target_pairs={{0,2},{1,3},{2,4},{3,5},{4,6},{5,7},{6,0},{7,1},{8,10},{9,11},{10,... | collective-permute-start | bytes 49160 | tf_op jit(solution)/shard_map/ppermute | solution.py:369
  (21 other events, 75.4 us)
where the time goes:
time: 104 us
  waiting for transfers between devices  37.7 us (36%)
  Pallas kernels  34.5 us (33%)
  starting transfers between devices  24.4 us (23%)
  local copies, waits for them, and re-layouts  6.39 us (6%)
    pallas_call x23, Pallas kernels, call(): pl.pallas_call(kernel, out_shape=[jax.ShapeDtypeStruct(x, jnp.float32) fo...  34.5 us
    ppermute x16, waiting for transfers between devices, on_device(): swap_b = lambda x: lax.ppermute(x, AXES, across)  33.2 us
    ppermute x16, starting transfers between devices, on_device(): swap_b = lambda x: lax.ppermute(x, AXES, across)  21.7 us
    unnamed x34, local copies, waits for them, and re-layouts  6.39 us
    ppermute x3, waiting for transfers between devices, sum_over_gz(): lax.ppermute(pair, 'gz', [(i, (i + 2 * k) % count) for i in range(count)])  3.26 us
  transfers between devices with their start and end apart: 36, of which 14 were waited for; matrix products, arithmetic and copies ran while one was open for 0% of the time, Pallas kernels for 18%

commit v1 on v0

v1 whole, which is shorter than its diff:
```python
import functools

import jax
import jax.numpy as jnp
from jax import lax
from jax.experimental import pallas as pl
from jax.experimental.pallas import tpu as pltpu
from jax.sharding import PartitionSpec as P


STEPS = 8
PAIRS = 4
ROWS = 8
LANES = 128
AXES = ("sample", "gz")
DOTS = [("s", i, j) for i in range(PAIRS) for j in range(i, PAIRS)] + [
    ("y", i, j) for i in range(PAIRS) for j in range(i, PAIRS)
]
DOT_ROWS = 32

VMEM = pl.BlockSpec(memory_space=pltpu.VMEM)


def near_plane():
    return lax.rem(lax.axis_index("gz"), 2)


def has_chip_neighbour():
    place = lax.axis_index("gz")
    edge = (place == 0) | (place == lax.axis_size("gz") - 1)
    return jnp.where(edge, 0.0, 1.0).astype(jnp.float32)


def mul(x, y):
    return [a * b for a, b in zip(x, y)]


def add(x, y):
    return [a + b for a, b in zip(x, y)]


def sub(x, y):
    return [a - b for a, b in zip(x, y)]


def scale(x, factor):
    return [a * factor for a in x]


def lanes_of(ref, index, tile):
    row = tile * ROWS if isinstance(tile, int) else pl.multiple_of(tile * ROWS, ROWS)
    count = ref.shape[-1] // LANES
    return [ref[(*index, pl.ds(row, ROWS), pl.ds(k * LANES, LANES))] for k in range(count)]


def store(ref, index, tile, values):
    row = tile * ROWS if isinstance(tile, int) else pl.multiple_of(tile * ROWS, ROWS)
    for k, value in enumerate(values):
        ref[(*index, pl.ds(row, ROWS), pl.ds(k * LANES, LANES))] = value


def along_y(x, lane):
    zero = jnp.zeros_like(x[0])
    after = x[1:] + [zero]
    before = [zero] + x[:-1]
    high = [pltpu.roll(jnp.where(lane == 0, a, h), LANES - 1, 1) for a, h in zip(after, x)]
    low = [pltpu.roll(jnp.where(lane == LANES - 1, b, h), 1, 1) for b, h in zip(before, x)]
    return high, low


def along_x(before, here, after, row):
    high = [pltpu.roll(jnp.where(row == 0, a, h), ROWS - 1, 0) for a, h in zip(after, here)]
    low = [pltpu.roll(jnp.where(row == ROWS - 1, b, h), 1, 0) for b, h in zip(before, here)]
    return high, low


def plane_update(centre, ici, d2d, quarter, row, lane):
    u = [centre(c, 0) for c in range(3)]
    i0, d0 = [ici(c, 0) for c in range(3)], [d2d(c, 0) for c in range(3)]
    v = [sub(i0[c], d0[c]) for c in range(3)]
    xv = [
        along_x(sub(ici(c, -1), d2d(c, -1)), v[c], sub(ici(c, 1), d2d(c, 1)), row)
        for c in range(2)
    ]
    xs = [along_x(centre(c, -1), u[c], centre(c, 1), row) for c in range(3)]
    ys = [along_y(u[c], lane) for c in range(3)]
    yv2 = along_y(v[2], lane)
    g2 = add(scale(v[0], quarter), scale(sub(*xs[1]), 0.25))
    yg2 = along_y(g2, lane)
    yxu2 = along_y(sub(*xs[2]), lane)
    twice = [scale(u[c], 2.0) for c in range(3)]
    zsum = [add(i0[c], d0[c]) for c in range(3)]
    xsum = [add(*xs[c]) for c in range(3)]
    ysum = [add(*ys[c]) for c in range(3)]
    lap = [sub(add(add(zsum[c], xsum[c]), ysum[c]), scale(u[c], 6.0)) for c in range(3)]
    grad_div = [
        add(sub(zsum[0], twice[0]), scale(add(sub(*xv[1]), sub(*yv2)), quarter)),
        add(
            sub(xsum[1], twice[1]),
            add(scale(sub(*xv[0]), quarter), scale(sub(*yxu2), 0.25)),
        ),
        add(sub(ysum[2], twice[2]), sub(*yg2)),
    ]
    return u, twice, grad_div, lap


REACH = {"h": 1, "p": 1, "f": 1, "q": 1, "pb": 0, "fb": 0, "cp": 0, "cf": 0}


def plan(names, starts, start, stop, total):
    def sides(t):
        if t in (0, total - 1):
            return None
        found = {}
        for name in names:
            parts = starts[name]
            held = {
                max(i for i, first in enumerate(parts) if first <= t + k)
                for k in range(-REACH[name], REACH[name] + 1)
            }
            if len(held) > 1:
                return None
            found[name] = held.pop()
        return found

    runs = []
    for t in range(start, stop):
        here = sides(t)
        if here is not None and runs and runs[-1][2] == here:
            runs[-1][1] = t + 1
        else:
            runs.append([t, t + 1, here])
    return runs


def step_kernel(step, far, starts, start, stop, total, wave_ref, *refs):
    names = list(starts)
    source = {}
    at = 0
    for name in names:
        source[name] = refs[at : at + len(starts[name])]
        at += len(starts[name])
    ca, cb, cf, src = refs[at : at + 4]
    out, corr_out, token = refs[-3:]
    near = near_plane()
    index = 1 - near if far else near
    quarter, present = near.astype(jnp.float32) * 0.5 - 0.25, has_chip_neighbour()
    wave = wave_ref[step]
    row = lax.broadcasted_iota(jnp.int32, (ROWS, LANES), 0)
    lane = lax.broadcasted_iota(jnp.int32, (ROWS, LANES), 1)
    zeros = [jnp.zeros((ROWS, LANES), jnp.float32)] * (out.shape[2] // LANES)

    def tile_body(t, where):
        def read(name, at, k):
            n = t + k
            if where is None:
                if n < 0 or n >= total:
                    return zeros
                part = max(i for i, first in enumerate(starts[name]) if first <= n)
            else:
                part = where[name]
            return lanes_of(source[name][part], at, n - starts[name][part])

        def reader(name):
            if name == "h":
                return lambda c, k: scale(read("h", (c,), k), present)
            return lambda c, k: read(name, (c,), k)

        three, older, sums = ("fpq", "fb", "cf") if far else ("phf", "pb", "cp")
        here, twice, grad_div, lap = plane_update(
            *(reader(name) for name in three), quarter, row, lane
        )
        a, b = lanes_of(ca, (index,), t), lanes_of(cb, (index,), t)
        force = scale(lanes_of(cf, (index,), t), wave)
        product = None if step == 0 else read(sums, (), 0)
        for c in range(3):
            term = mul(here[c], lap[c])
            product = term if product is None else add(product, term)
            new = sub(twice[c], read(older, (c,), 0))
            new = add(new, mul(force, lanes_of(src, (c, index), t)))
            new = add(new, add(mul(a, grad_div[c]), mul(b, lap[c])))
            store(out, (c,), t - start, new)
        store(corr_out, (), t - start, product)

    for first, end, where in plan(names, starts, start, stop, total):
        if end - first < 3:
            for t in range(first, end):
                tile_body(t, where)
        else:

            def loop(t, carry, where=where):
                tile_body(t, where)
                return carry

            lax.fori_loop(first, end, loop, 0, unroll=UNROLL)
    token[...] = jnp.zeros(token.shape, jnp.float32)


UNROLL = 4


def step_call(step, far, start, stop, total, held, wave, fixed, tokens):
    starts = {key: [first for first, _ in parts] for key, parts in held.items()}
    arrays = [array for parts in held.values() for _, array in parts]
    cols = arrays[0].shape[-1]
    rows = (stop - start) * ROWS
    return call(
        functools.partial(step_kernel, step, far, starts, start, stop, total),
        [(3, rows, cols), (rows, cols), (ROWS, LANES)],
        [wave, *arrays, *fixed, *tokens],
        rows * cols * 120,
    )


VMEM_LIMIT = 20 * 2**20


def split_kernel(cut, u, low, high, far):
    near = near_plane()
    rows = u.shape[2]
    for c in range(3):
        low[c] = u[c, near, pl.ds(0, cut), :]
        high[c] = u[c, near, pl.ds(cut, rows - cut), :]
        far[c] = u[c, 1 - near]


def join_kernel(p_low, p_high, f, c_low, c_high, c_f, mu, prior, out, grad):
    near = near_plane()
    cut, rest = p_low.shape[1], p_high.shape[1]
    low, high = pl.ds(0, cut), pl.ds(cut, rest)
    for c in range(3):
        out[c, near, low, :] = p_low[c]
        out[c, near, high, :] = p_high[c]
        out[c, 1 - near] = f[c]
    grad[near, low, :] = (mu[near, low, :] - prior[near, low, :]) + 0.02 * c_low[...]
    grad[near, high, :] = (mu[near, high, :] - prior[near, high, :]) + 0.02 * c_high[...]
    grad[1 - near] = (mu[1 - near] - prior[1 - near]) + 0.02 * c_f[...]


def coeff_kernel(lam, mu, rho, ca, cb, cf):
    rows = lam.shape[1] // ROWS

    def loop(t, carry):
        r = pl.ds(pl.multiple_of(t * ROWS, ROWS), ROWS)
        for d in range(lam.shape[0]):
            coeff = 0.04 / rho[d, r, :]
            m = mu[d, r, :]
            ca[d, r, :] = coeff * (lam[d, r, :] + m)
            cb[d, r, :] = coeff * m
            cf[d, r, :] = coeff
        return carry

    lax.fori_loop(0, rows, loop, 0)


def dots_kernel(s, y, out):
    depth, rows, cols = s.shape[1:]
    count = len(DOTS)

    def loop(t, sums):
        r = pl.ds(pl.multiple_of(t * ROWS, ROWS), ROWS)
        sums = list(sums)
        for d in range(depth):
            for k in range(cols // LANES):
                at = (d, r, pl.ds(k * LANES, LANES))
                vs = [s[(i, *at)] for i in range(PAIRS)]
                vy = [y[(i, *at)] for i in range(PAIRS)]
                for n, (kind, i, j) in enumerate(DOTS):
                    sums[n] = sums[n] + (vs[i] if kind == "s" else vy[i]) * vy[j]
        return tuple(sums)

    zero = jnp.zeros((ROWS, LANES), jnp.float32)
    sums = lax.fori_loop(0, rows // ROWS, loop, (zero,) * count)
    out[...] = jnp.zeros(out.shape, jnp.float32)
    for n in range(count):
        out[pl.ds(n, 1), :] = jnp.sum(sums[n], axis=0, keepdims=True)


def gradient_dots_kernel(parts, mu, prior, s, y, so_far, *refs):
    out = refs[-1]
    cols = mu.shape[2]
    sums = (jnp.zeros((ROWS, LANES), jnp.float32),) * (2 * PAIRS)
    for (far, base), corr in zip(parts, refs):
        index = 1 - near_plane() if far else near_plane()

        def loop(t, sums, corr=corr, base=base, index=index):
            sums = list(sums)
            r = pl.ds(pl.multiple_of((base + t) * ROWS, ROWS), ROWS)
            r_corr = pl.ds(pl.multiple_of(t * ROWS, ROWS), ROWS)
            for k in range(cols // LANES):
                lanes = pl.ds(k * LANES, LANES)
                at = (index, r, lanes)
                g = (mu[at] - prior[at]) + 0.02 * corr[r_corr, lanes]
                for i in range(PAIRS):
                    sums[i] = sums[i] + s[(i, *at)] * g
                    sums[PAIRS + i] = sums[PAIRS + i] + y[(i, *at)] * g
            return tuple(sums)

        sums = lax.fori_loop(0, corr.shape[0] // ROWS, loop, sums, unroll=2)
    out[...] = so_far[...]
    for n in range(2 * PAIRS):
        at = pl.ds(len(DOTS) + n, 1)
        out[at, :] = so_far[at, :] + jnp.sum(sums[n], axis=0, keepdims=True)


def direction_kernel(parts, grad, s, y, out):
    depth, rows, cols = grad.shape
    dots = parts[0]
    for n in range(1, parts.shape[0]):
        dots = dots + parts[n]
    shift = LANES // 2
    while shift:
        dots = dots + pltpu.roll(dots, shift, 1)
        shift //= 2
    value = {}
    for n, key in enumerate(DOTS):
        value[key] = dots[n : n + 1, :]
    for i in range(PAIRS):
        value["sg", i] = dots[len(DOTS) + i : len(DOTS) + i + 1, :]
        value["yg", i] = dots[len(DOTS) + PAIRS + i : len(DOTS) + PAIRS + i + 1, :]
    rho = [1.0 / value["s", i, i] for i in range(PAIRS)]
    alpha = [None] * PAIRS
    for i in reversed(range(PAIRS)):
        inner = value["sg", i]
        for j in range(i + 1, PAIRS):
            inner = inner - alpha[j] * value["s", i, j]
        alpha[i] = rho[i] * inner
    last = PAIRS - 1
    gamma = value["s", last, last] / value["y", last, last]
    step = [None] * PAIRS
    for i in range(PAIRS):
        inner = value["yg", i]
        for j in range(PAIRS):
            inner = inner - alpha[j] * value["y", min(i, j), max(i, j)]
        inner = gamma * inner
        for j in range(i):
            inner = inner + step[j] * value["s", j, i]
        step[i] = alpha[i] - rho[i] * inner
    wide = lambda x: jnp.broadcast_to(x, (ROWS, LANES))
    by_g = wide(-gamma)
    by_y = [wide(gamma * a) for a in alpha]
    by_s = [wide(-b) for b in step]

    def loop(t, carry):
        r = pl.ds(pl.multiple_of(t * ROWS, ROWS), ROWS)
        for d in range(depth):
            for k in range(cols // LANES):
                at = (d, r, pl.ds(k * LANES, LANES))
                total = by_g * grad[at]
                for i in range(PAIRS):
                    total = total + by_y[i] * y[(i, *at)] + by_s[i] * s[(i, *at)]
                out[at] = total
        return carry

    lax.fori_loop(0, rows // ROWS, loop, 0)


def call(kernel, out_shape, operands, flops):
    return pl.pallas_call(
        kernel,
        out_shape=[jax.ShapeDtypeStruct(x, jnp.float32) for x in out_shape],
        in_specs=[VMEM] * len(operands),
        out_specs=[VMEM] * len(out_shape),
        compiler_params=pltpu.CompilerParams(vmem_limit_bytes=VMEM_LIMIT),
        cost_estimate=pl.CostEstimate(flops=flops, bytes_accessed=0, transcendentals=0),
    )(*operands)


def pairings():
    samples, count = lax.axis_size("sample"), lax.axis_size("gz")
    inside = [(i, i ^ 1) for i in range(count)]
    across = []
    for sample in range(samples):
        for i in range(1, count - 1, 2):
            across += [(sample * count + i, sample * count + i + 1)]
            across += [(sample * count + i + 1, sample * count + i)]
        partner = sample ^ 1 if samples % 2 == 0 else sample
        for i in (0, count - 1):
            across.append((sample * count + i, partner * count + i))
    return inside, across


def sum_over_gz(part):
    count = lax.axis_size("gz")
    pair = part + lax.ppermute(part, "gz", [(i, i ^ 1) for i in range(count)])
    if count > 8:
        return lax.psum(part, "gz")[None]
    parts = [pair]
    for k in range(1, count // 2):
        parts.append(lax.ppermute(pair, "gz", [(i, (i + 2 * k) % count) for i in range(count)]))
    return jnp.stack(parts)


def on_device(
    field_now,
    field_before,
    lame_lambda,
    shear_modulus,
    density,
    source_field,
    wavelet,
    prior_mean,
    steps_taken,
    grad_change,
):
    depth, rows, cols = shear_modulus.shape
    count = lax.axis_size("gz")
    assert depth == 2 and count % 2 == 0
    inside, across = pairings()
    total = rows // ROWS
    cells = shear_modulus.size
    cuts = [total // 2 + STEPS // 2 - n for n in range(STEPS + 1)]
    wave = jnp.broadcast_to(wavelet[:, None, None], (STEPS, ROWS, LANES))

    def cut_planes(field, tiles):
        cut = tiles * ROWS
        shapes = [(3, cut, cols), (3, rows - cut, cols), (3, rows, cols)]
        low, high, far = call(functools.partial(split_kernel, cut), shapes, [field], cells)
        return [(0, low), (tiles, high)], [(0, far)]

    def across_chips(x):
        return lax.ppermute(x, AXES, across)

    def across_cores(x):
        return lax.ppermute(x, "gz", inside)

    near_now, far_now = cut_planes(field_now, cuts[0])
    ghosts = [(first, across_chips(x)) for first, x in near_now]
    partner = [(0, across_cores(far_now[0][1]))]
    near_old, far_old = cut_planes(field_before, cuts[0] + 1)
    fixed = call(
        coeff_kernel, [shear_modulus.shape] * 3, [lame_lambda, shear_modulus, density], cells * 10
    )
    fixed = list(fixed) + [source_field]
    (static,) = call(dots_kernel, [(DOT_ROWS, LANES)], [steps_taken, grad_change], cells * 40)
    near_sum = far_sum = None
    for n in range(STEPS):
        last = n == STEPS - 1
        middle = cuts[n + 1]
        held = {"f": far_now, "p": near_now, "q": partner, "fb": far_old}
        held |= {} if n == 0 else {"cf": far_sum}
        new_far, sum_far, token = step_call(n, True, 0, total, total, held, wave, fixed, [])
        if not last:
            partner = [(0, across_cores(new_far))]
        held = {"p": near_now[:1], "h": ghosts[:1], "f": far_now, "pb": near_old[:1]}
        held |= {} if n == 0 else {"cp": near_sum[:1]}
        new_low, sum_low, token = step_call(n, False, 0, middle, total, held, wave, fixed, [token])
        if not last:
            low_ghost = across_chips(new_low)
        held = {"p": near_now, "h": ghosts, "f": far_now, "pb": near_old}
        held |= {} if n == 0 else {"cp": near_sum}
        new_high, sum_high, _ = step_call(
            n, False, middle, total, total, held, wave, fixed, [token]
        )
        if not last:
            ghosts = [(0, low_ghost), (middle, across_chips(new_high))]
        near_old, far_old = near_now, far_now
        near_now, far_now = [(0, new_low), (middle, new_high)], [(0, new_far)]
        near_sum, far_sum = [(0, sum_low), (middle, sum_high)], [(0, sum_far)]

    def gradient_dots(so_far, parts):
        operands = [shear_modulus, prior_mean, steps_taken, grad_change, so_far]
        where = [(far, first) for far, first, _ in parts]
        (out,) = call(
            functools.partial(gradient_dots_kernel, where),
            [(DOT_ROWS, LANES)],
            operands + [x for *_, x in parts],
            cells * 20,
        )
        return out

    early = gradient_dots(static, [(True, 0, sum_far), (False, 0, sum_low)])
    mine = gradient_dots(early, [(False, middle, sum_high)])
    final, gradient = call(
        join_kernel,
        [field_now.shape, shear_modulus.shape],
        [new_low, new_high, new_far, sum_low, sum_high, sum_far, shear_modulus, prior_mean],
        cells,
    )
    parts = sum_over_gz(mine)
    (direction,) = call(
        direction_kernel,
        [shear_modulus.shape],
        [parts, gradient, steps_taken, grad_change],
        cells * 20,
    )
    return (final, gradient, direction)


def solution(mesh):
    placed = (
        P("sample", "gz", None, None),
        P("sample", "gz", None, None),
        P("gz", "sample", None),
        P("gz", "sample", None),
        P("gz", "sample", None),
        P("sample", "gz", None, None),
        P("sample"),
        P("gz", "sample", None),
        P("sample", "gz", None, None),
        P("sample", "gz", None, None),
    )
    return jax.shard_map(
        on_device,
        mesh=mesh,
        in_specs=placed,
        out_specs=(P("sample", "gz", None, None), P("gz", "sample", None), P("gz", "sample", None)),
        check_vma=False,
    )
```

time: 104 us -> 107 us (1.029)
  waiting for transfers between devices: 37.7 us -> 50.4 us
  Pallas kernels: 34.5 us -> 26.2 us
  starting transfers between devices: 24.4 us -> 22.7 us
    ppermute x32 -> x24, waiting for transfers between devices: 33.2 us -> 48.2 us  [the longest x16 48.1 us: across_chips(): return lax.ppermute(x, AXES, across)]
    pallas_call x23 -> x32, Pallas kernels: 34.5 us -> 26.2 us  [call(): pl.pallas_call(kernel, out_shape=[jax.ShapeDtypeStruct(x, jnp.float32) fo...]
    ppermute x32 -> x24, starting transfers between devices: 22.3 us -> 18.8 us  [the longest x16 17.2 us: across_chips(): return lax.ppermute(x, AXES, across)]
    ppermute x3, waiting for transfers between devices: 3.26 us -> 1.11 us  [sum_over_gz(): lax.ppermute(pair, 'gz', [(i, (i + 2 * k) % count) for i in range(count)])]
    ppermute x3, starting transfers between devices: 2.03 us -> 3.82 us  [sum_over_gz(): lax.ppermute(pair, 'gz', [(i, (i + 2 * k) % count) for i in range(count)])]
    unnamed x34 -> x22, local copies, waits for them, and re-layouts: 6.39 us -> 6.16 us
  transfers between devices with their start and end apart: 36 -> 28, of which waited for: 14 -> 16; matrix products, arithmetic and copies ran while one was open for 0% -> 0% of each run, Pallas kernels for 18% -> 15%
where the time goes in v1:
time: 107 us
  waiting for transfers between devices  50.4 us (47%)
  Pallas kernels  26.2 us (24%)
  starting transfers between devices  22.7 us (21%)
  local copies, waits for them, and re-layouts  6.23 us (6%)
    ppermute x16, waiting for transfers between devices, across_chips(): return lax.ppermute(x, AXES, across)  48.1 us
    pallas_call x32, Pallas kernels, call(): pl.pallas_call(kernel, out_shape=[jax.ShapeDtypeStruct(x, jnp.float32) fo...  26.2 us
    ppermute x16, starting transfers between devices, across_chips(): return lax.ppermute(x, AXES, across)  17.2 us
    unnamed x22, local copies, waits for them, and re-layouts  6.16 us
    ppermute x3, starting transfers between devices, sum_over_gz(): lax.ppermute(pair, 'gz', [(i, (i + 2 * k) % count) for i in range(count)])  3.82 us
  transfers between devices with their start and end apart: 28, of which 16 were waited for; matrix products, arithmetic and copies ran while one was open for 0% of the time, Pallas kernels for 15%

profile of v1, /device:TPU:0, one launch (start us, length us, event | category | flops | bytes accessed | tf_op | source)
XLA Modules:
  0.0 106.5 jit_solution(6540398230996109289)
XLA Ops:
  0.7 1.3 %copy-done.5 = f32[3,2,160,256]{3,2,1,0:T(8,128)S(1)} copy-done((f32[3,2,160,256]{3,2,1,0:T(8,128)S(1)}, f32[3,2,160,256]{3,2,1,0:T(8,128)}, u32[]{:S(2)}) %copy-start.5) | copy-done | bytes 983064
  2.6 1.2 %copy-done.6 = f32[3,2,160,256]{3,2,1,0:T(8,128)S(1)} copy-done((f32[3,2,160,256]{3,2,1,0:T(8,128)S(1)}, f32[3,2,160,256]{3,2,1,0:T(8,128)}, u32[]{:S(2)}) %copy-start.6) | copy-done | bytes 983064
  7.2 3.0 %collective-permute-start = (f32[3,112,256]{2,1,0:T(8,128)S(1)}, f32[3,112,256]{2,1,0:T(8,128)S(1)}, u32[]{:S(2)}, u32[]{:S(2)}) collective-permute-start(f32[3,112,256]{2,1,0:T(8,128)S(1)} %get-tuple-element.78.refs_1_.refs_0_.refs_3_.refs_5_), channel_id=1, source_target_pairs={{1,2},{2,1},{3,4},{4,3},{5,6},{6,5},{0,8},{7,15},{9,10},{10,9},{11... | collective-permute-start | bytes 1032200 | tf_op jit(solution)/shard_map/ppermute | solution.py:422
  10.2 5.2 %collective-permute-done.refs_1_.refs_2_ = f32[3,112,256]{2,1,0:T(8,128)S(1)} collective-permute-done((f32[3,112,256]{2,1,0:T(8,128)S(1)}, f32[3,112,256]{2,1,0:T(8,128)S(1)}, u32[]{:S(2)}, u32[]{:S(2)}) %collective-permute-start) | collective-permute-done | bytes 344096 | tf_op jit(solution)/shard_map/ppermute | solution.py:422
  19.0 2.0 %collective-permute-start.2 = (f32[3,104,256]{2,1,0:T(8,128)S(1)}, f32[3,104,256]{2,1,0:T(8,128)S(1)}, u32[]{:S(2)}, u32[]{:S(2)}) collective-permute-start(f32[3,104,256]{2,1,0:T(8,128)S(1)} %get-tuple-element.87.refs_1_.refs_0_.refs_3_.refs_5_), channel_id=1, source_target_pairs={{1,2},{2,1},{3,4},{4,3},{5,6},{6,5},{0,8},{7,15},{9,10},{10,9},{11... | collective-permute-start | bytes 958472 | tf_op jit(solution)/shard_map/ppermute | solution.py:422
  21.1 4.9 %collective-permute-done.2.refs_1_.refs_2_ = f32[3,104,256]{2,1,0:T(8,128)S(1)} collective-permute-done((f32[3,104,256]{2,1,0:T(8,128)S(1)}, f32[3,104,256]{2,1,0:T(8,128)S(1)}, u32[]{:S(2)}, u32[]{:S(2)}) %collective-permute-start.2) | collective-permute-done | bytes 319520 | tf_op jit(solution)/shard_map/ppermute | solution.py:422
  28.8 1.2 %shard_map.130 = (f32[3,160,256]{2,1,0:T(8,128)S(1)}, f32[160,256]{1,0:T(8,128)S(1)}, f32[8,128]{1,0:T(8,128)S(1)}) custom-call(f32[8,8,128]{2,1,0:T(8,128)S(1)} %broadcast_in_dim.2.wave_ref, f32[3,160,256]{2,1,0:T(8,128)S(1)} %get-tuple-element.96.refs_0_.refs_2_.refs_4_, f32[3,96,256]{2,1,0:T(8,128)S(1)} %get-tuple-element.95.refs_1_.refs_0_.refs_3_.refs_5_, ...), custom_call_target="tpu_custom_call" | custom-call | flops 4915200 | tf_op jit(solution)/shard_map/pallas_call | solution.py:359
  30.2 2.0 %collective-permute-start.5 = (f32[3,96,256]{2,1,0:T(8,128)S(1)}, f32[3,96,256]{2,1,0:T(8,128)S(1)}, u32[]{:S(2)}, u32[]{:S(2)}) collective-permute-start(f32[3,96,256]{2,1,0:T(8,128)S(1)} %get-tuple-element.95.refs_1_.refs_0_.refs_3_.refs_5_), channel_id=1, source_target_pairs={{1,2},{2,1},{3,4},{4,3},{5,6},{6,5},{0,8},{7,15},{9,10},{10,9},{11... | collective-permute-start | bytes 884744 | tf_op jit(solution)/shard_map/ppermute | solution.py:422
  32.2 4.7 %collective-permute-done.5.refs_1_.refs_2_ = f32[3,96,256]{2,1,0:T(8,128)S(1)} collective-permute-done((f32[3,96,256]{2,1,0:T(8,128)S(1)}, f32[3,96,256]{2,1,0:T(8,128)S(1)}, u32[]{:S(2)}, u32[]{:S(2)}) %collective-permute-start.5) | collective-permute-done | bytes 294944 | tf_op jit(solution)/shard_map/ppermute | solution.py:422
  37.5 1.4 %collective-permute-done.9.refs_3_ = f32[3,64,256]{2,1,0:T(8,128)S(1)} collective-permute-done((f32[3,64,256]{2,1,0:T(8,128)S(1)}, f32[3,64,256]{2,1,0:T(8,128)S(1)}, u32[]{:S(2)}, u32[]{:S(2)}) %collective-permute-start.9) | collective-permute-done | bytes 196640 | tf_op jit(solution)/shard_map/ppermute | solution.py:422
  40.0 1.2 %shard_map.133 = (f32[3,160,256]{2,1,0:T(8,128)S(1)}, f32[160,256]{1,0:T(8,128)S(1)}, f32[8,128]{1,0:T(8,128)S(1)}) custom-call(f32[8,8,128]{2,1,0:T(8,128)S(1)} %broadcast_in_dim.2.wave_ref, f32[3,160,256]{2,1,0:T(8,128)S(1)} %get-tuple-element.104.refs_0_.refs_2_.refs_4_, f32[3,88,256]{2,1,0:T(8,128)S(1)} %get-tuple-element.103.refs_1_.refs_0_.refs_3_.refs_5_, ...), custom_call_target="tpu_custom_call" | custom-call | flops 4915200 | tf_op jit(solution)/shard_map/pallas_call | solution.py:359
  41.4 2.0 %collective-permute-start.8 = (f32[3,88,256]{2,1,0:T(8,128)S(1)}, f32[3,88,256]{2,1,0:T(8,128)S(1)}, u32[]{:S(2)}, u32[]{:S(2)}) collective-permute-start(f32[3,88,256]{2,1,0:T(8,128)S(1)} %get-tuple-element.103.refs_1_.refs_0_.refs_3_.refs_5_), channel_id=1, source_target_pairs={{1,2},{2,1},{3,4},{4,3},{5,6},{6,5},{0,8},{7,15},{9,10},{10,9},{11... | collective-permute-start | bytes 811016 | tf_op jit(solution)/shard_map/ppermute | solution.py:422
  43.4 4.4 %collective-permute-done.8.refs_1_.refs_2_ = f32[3,88,256]{2,1,0:T(8,128)S(1)} collective-permute-done((f32[3,88,256]{2,1,0:T(8,128)S(1)}, f32[3,88,256]{2,1,0:T(8,128)S(1)}, u32[]{:S(2)}, u32[]{:S(2)}) %collective-permute-start.8) | collective-permute-done | bytes 270368 | tf_op jit(solution)/shard_map/ppermute | solution.py:422
  48.4 1.8 %collective-permute-done.12.refs_3_ = f32[3,72,256]{2,1,0:T(8,128)S(1)} collective-permute-done((f32[3,72,256]{2,1,0:T(8,128)S(1)}, f32[3,72,256]{2,1,0:T(8,128)S(1)}, u32[]{:S(2)}, u32[]{:S(2)}) %collective-permute-start.12) | collective-permute-done | bytes 221216 | tf_op jit(solution)/shard_map/ppermute | solution.py:422
  50.2 1.2 %shard_map.135 = (f32[3,80,256]{2,1,0:T(8,128)S(1)}, f32[80,256]{1,0:T(8,128)S(1)}, f32[8,128]{1,0:T(8,128)}) custom-call(f32[8,8,128]{2,1,0:T(8,128)S(1)} %broadcast_in_dim.2.wave_ref, f32[3,88,256]{2,1,0:T(8,128)S(1)} %get-tuple-element.103.refs_1_.refs_0_.refs_3_.refs_5_, f32[3,72,256]{2,1,0:T(8,128)S(1)} %get-tuple-element.108.refs_2_.refs_1_.refs_6_, ...), custom_call_target="tpu_custom_call" | custom-call | flops 2457600 | tf_op jit(solution)/shard_map/pallas_call | solution.py:359
  52.6 2.0 %collective-permute-start.11 = (f32[3,80,256]{2,1,0:T(8,128)S(1)}, f32[3,80,256]{2,1,0:T(8,128)S(1)}, u32[]{:S(2)}, u32[]{:S(2)}) collective-permute-start(f32[3,80,256]{2,1,0:T(8,128)S(1)} %get-tuple-element.111.refs_1_.refs_0_.refs_3_.refs_5_), channel_id=1, source_target_pairs={{1,2},{2,1},{3,4},{4,3},{5,6},{6,5},{0,8},{7,15},{9,10},{10,9},{11... | collective-permute-start | bytes 737288 | tf_op jit(solution)/shard_map/ppermute | solution.py:422
  54.6 4.2 %collective-permute-done.11.refs_1_.refs_2_ = f32[3,80,256]{2,1,0:T(8,128)S(1)} collective-permute-done((f32[3,80,256]{2,1,0:T(8,128)S(1)}, f32[3,80,256]{2,1,0:T(8,128)S(1)}, u32[]{:S(2)}, u32[]{:S(2)}) %collective-permute-start.11) | collective-permute-done | bytes 245792 | tf_op jit(solution)/shard_map/ppermute | solution.py:422
  59.3 2.2 %collective-permute-done.15.refs_3_ = f32[3,80,256]{2,1,0:T(8,128)S(1)} collective-permute-done((f32[3,80,256]{2,1,0:T(8,128)S(1)}, f32[3,80,256]{2,1,0:T(8,128)S(1)}, u32[]{:S(2)}, u32[]{:S(2)}) %collective-permute-start.15) | collective-permute-done | bytes 245792 | tf_op jit(solution)/shard_map/ppermute | solution.py:422
  63.9 2.0 %collective-permute-start.18 = (f32[3,88,256]{2,1,0:T(8,128)S(1)}, f32[3,88,256]{2,1,0:T(8,128)S(1)}, u32[]{:S(2)}, u32[]{:S(2)}) collective-permute-start(f32[3,88,256]{2,1,0:T(8,128)S(1)} %get-tuple-element.124.refs_2_.refs_1_.refs_6_), channel_id=1, source_target_pairs={{1,2},{2,1},{3,4},{4,3},{5,6},{6,5},{0,8},{7,15},{9,10},{10,9},{11... | collective-permute-start | bytes 811016 | tf_op jit(solution)/shard_map/ppermute | solution.py:422
  65.9 6.8 %collective-permute-done.14.refs_1_.refs_2_ = f32[3,72,256]{2,1,0:T(8,128)S(1)} collective-permute-done((f32[3,72,256]{2,1,0:T(8,128)S(1)}, f32[3,72,256]{2,1,0:T(8,128)S(1)}, u32[]{:S(2)}, u32[]{:S(2)}) %collective-permute-start.14) | collective-permute-done | bytes 221216 | tf_op jit(solution)/shard_map/ppermute | solution.py:422
  73.2 1.2 %shard_map.141 = (f32[3,96,256]{2,1,0:T(8,128)S(1)}, f32[96,256]{1,0:T(8,128)S(1)}, f32[8,128]{1,0:T(8,128)}) custom-call(f32[8,8,128]{2,1,0:T(8,128)S(1)} %broadcast_in_dim.2.wave_ref, f32[3,72,256]{2,1,0:T(8,128)S(1)} %get-tuple-element.119.refs_1_.refs_0_.refs_3_.refs_5_, f32[3,88,256]{2,1,0:T(8,128)S(1)} %get-tuple-element.124.refs_2_.refs_1_.refs_6_, ...), custom_call_target="tpu_custom_call" | custom-call | flops 2949120 | tf_op jit(solution)/shard_map/pallas_call | solution.py:359
  74.4 2.0 %collective-permute-start.21 = (f32[3,96,256]{2,1,0:T(8,128)S(1)}, f32[3,96,256]{2,1,0:T(8,128)S(1)}, u32[]{:S(2)}, u32[]{:S(2)}) collective-permute-start(f32[3,96,256]{2,1,0:T(8,128)S(1)} %get-tuple-element.132.refs_2_.refs_1_.refs_6_), channel_id=1, source_target_pairs={{1,2},{2,1},{3,4},{4,3},{5,6},{6,5},{0,8},{7,15},{9,10},{10,9},{11... | collective-permute-start | bytes 884744 | tf_op jit(solution)/shard_map/ppermute | solution.py:422
  76.4 1.2 %shard_map.142 = (f32[3,160,256]{2,1,0:T(8,128)S(1)}, f32[160,256]{1,0:T(8,128)S(1)}, f32[8,128]{1,0:T(8,128)S(1)}) custom-call(f32[8,8,128]{2,1,0:T(8,128)S(1)} %broadcast_in_dim.2.wave_ref, f32[3,160,256]{2,1,0:T(8,128)S(1)} %get-tuple-element.128.refs_0_.refs_2_.refs_4_, f32[3,64,256]{2,1,0:T(8,128)S(1)} %get-tuple-element.127.refs_1_.refs_0_.refs_3_.refs_5_, ...), custom_call_target="tpu_custom_call" | custom-call | flops 4915200 | tf_op jit(solution)/shard_map/pallas_call | solution.py:359
  77.7 5.5 %collective-permute-done.17.refs_1_.refs_2_ = f32[3,64,256]{2,1,0:T(8,128)S(1)} collective-permute-done((f32[3,64,256]{2,1,0:T(8,128)S(1)}, f32[3,64,256]{2,1,0:T(8,128)S(1)}, u32[]{:S(2)}, u32[]{:S(2)}) %collective-permute-start.17) | collective-permute-done | bytes 196640 | tf_op jit(solution)/shard_map/ppermute | solution.py:422
  83.7 1.3 %shard_map.144 = (f32[3,104,256]{2,1,0:T(8,128)S(1)}, f32[104,256]{1,0:T(8,128)S(1)}, f32[8,128]{1,0:T(8,128)}) custom-call(f32[8,8,128]{2,1,0:T(8,128)S(1)} %broadcast_in_dim.2.wave_ref, f32[3,64,256]{2,1,0:T(8,128)S(1)} %get-tuple-element.127.refs_1_.refs_0_.refs_3_.refs_5_, f32[3,96,256]{2,1,0:T(8,128)S(1)} %get-tuple-element.132.refs_2_.refs_1_.refs_6_, ...), custom_call_target="tpu_custom_call" | custom-call | flops 3194880 | tf_op jit(solution)/shard_map/pallas_call | solution.py:359
  85.0 2.0 %collective-permute-start.23 = (f32[3,104,256]{2,1,0:T(8,128)S(1)}, f32[3,104,256]{2,1,0:T(8,128)S(1)}, u32[]{:S(2)}, u32[]{:S(2)}) collective-permute-start(f32[3,104,256]{2,1,0:T(8,128)S(1)} %get-tuple-element.140.refs_2_.refs_1_), channel_id=1, source_target_pairs={{1,2},{2,1},{3,4},{4,3},{5,6},{6,5},{0,8},{7,15},{9,10},{10,9},{11... | collective-permute-start | bytes 958472 | tf_op jit(solution)/shard_map/ppermute | solution.py:422
  88.8 5.1 %collective-permute-done.20.refs_1_.refs_2_ = f32[3,56,256]{2,1,0:T(8,128)S(1)} collective-permute-done((f32[3,56,256]{2,1,0:T(8,128)S(1)}, f32[3,56,256]{2,1,0:T(8,128)S(1)}, u32[]{:S(2)}, u32[]{:S(2)}) %collective-permute-start.20) | collective-permute-done | bytes 172064 | tf_op jit(solution)/shard_map/ppermute | solution.py:422
  95.0 1.4 %shard_map.147 = (f32[3,112,256]{2,1,0:T(8,128)S(1)}, f32[112,256]{1,0:T(8,128)S(1)}, f32[8,128]{1,0:T(8,128)}) custom-call(f32[8,8,128]{2,1,0:T(8,128)S(1)} %broadcast_in_dim.2.wave_ref, f32[3,56,256]{2,1,0:T(8,128)S(1)} %get-tuple-element.135.refs_1_.refs_0_, f32[3,104,256]{2,1,0:T(8,128)S(1)} %get-tuple-element.140.refs_2_.refs_1_, ...), custom_call_target="tpu_custom_call" | custom-call | flops 3440640 | tf_op jit(solution)/shard_map/pallas_call | solution.py:359
  96.7 1.2 %collective-permute-done.24 = f32[32,128]{1,0:T(8,128)S(1)} collective-permute-done((f32[32,128]{1,0:T(8,128)S(1)}, f32[32,128]{1,0:T(8,128)S(1)}, u32[]{:S(2)}, u32[]{:S(2)}) %collective-permute-start.24) | collective-permute-done | bytes 16416 | tf_op jit(solution)/shard_map/ppermute | solution.py:385
  97.9 3.7 %collective-permute-start.27 = (f32[32,128]{1,0:T(8,128)S(1)}, f32[32,128]{1,0:T(8,128)S(1)}, u32[]{:S(2)}, u32[]{:S(2)}) collective-permute-start(f32[32,128]{1,0:T(8,128)S(1)} %add.3), channel_id=1, source_target_pairs={{0,6},{1,7},{2,0},{3,1},{4,2},{5,3},{6,4},{7,5},{8,14},{9,15},{10,... | collective-permute-start | bytes 49160 | tf_op jit(solution)/shard_map/ppermute | solution.py:390
  101.7 1.2 %shard_map.148 = (f32[3,2,160,256]{3,2,1,0:T(8,128)}, f32[2,160,256]{2,1,0:T(8,128)}) custom-call(f32[3,48,256]{2,1,0:T(8,128)S(1)} %get-tuple-element.143.p_low, f32[3,112,256]{2,1,0:T(8,128)S(1)} %get-tuple-element.146.p_high, f32[3,160,256]{2,1,0:T(8,128)S(1)} %get-tuple-element.147.f, f32[48,256]{1,0:T(8,128)S(1)} %get-tuple-element.148.c_low.refs_1_, ...), custom_call_target="tpu_custom_call" | custom-call | flops 81920 | tf_op jit(solution)/shard_map/pallas_call | solution.py:359
  104.9 1.6 %shard_map.152 = f32[2,160,256]{2,1,0:T(8,128)} custom-call(f32[4,32,128]{2,1,0:T(8,128)S(1)} %pad_maximum_fusion.parts, f32[2,160,256]{2,1,0:T(8,128)S(1)} %copy-done.7, f32[4,2,160,256]{3,2,1,0:T(8,128)S(1)} %copy-done.1, f32[4,2,160,256]{3,2,1,0:T(8,128)S(1)} %copy-done.2), custom_call_target="tpu_custom_call" | custom-call | flops 1638400 | tf_op jit(solution)/shard_map/pallas_call | solution.py:359
  (81 shorter events, 23.8 us)
Async XLA Ops:
  0.6 3.2 %copy-start.3 = (f32[2,160,256]{2,1,0:T(8,128)S(1)}, f32[2,160,256]{2,1,0:T(8,128)}, u32[]{:S(2)}) copy-start(f32[2,160,256]{2,1,0:T(8,128)} %mu.7) | copy-start | bytes 983044
  0.6 5.5 %copy-start = (f32[3,2,160,256]{3,2,1,0:T(8,128)S(1)}, f32[3,2,160,256]{3,2,1,0:T(8,128)}, u32[]{:S(2)}) copy-start(f32[3,2,160,256]{3,2,1,0:T(8,128)} %refs_12_.13) | copy-start | bytes 2949124
  2.0 4.0 %collective-permute-start.1 = (f32[3,160,256]{2,1,0:T(8,128)S(1)}, f32[3,160,256]{2,1,0:T(8,128)S(1)}, u32[]{:S(2)}, u32[]{:S(2)}) collective-permute-start(f32[3,160,256]{2,1,0:T(8,128)S(1)} %get-tuple-element.79.refs_0_.refs_2_.refs_4_), channel_id=1, source_target_pairs={{0,1},{1,0},{2,3},{3,2},{4,5},{5,4},{6,7},{7,6},{8,9},{9,8},{10,11... | collective-permute-start | bytes 1474568 | tf_op jit(solution)/shard_map/ppermute | solution.py:425
  7.1 10.7 %collective-permute-start.4 = (f32[3,160,256]{2,1,0:T(8,128)S(1)}, f32[3,160,256]{2,1,0:T(8,128)S(1)}, u32[]{:S(2)}, u32[]{:S(2)}) collective-permute-start(f32[3,160,256]{2,1,0:T(8,128)S(1)} %get-tuple-element.88.refs_0_.refs_2_.refs_4_), channel_id=1, source_target_pairs={{0,1},{1,0},{2,3},{3,2},{4,5},{5,4},{6,7},{7,6},{8,9},{9,8},{10,11... | collective-permute-start | bytes 1474568 | tf_op jit(solution)/shard_map/ppermute | solution.py:425
  7.2 8.2 %collective-permute-start = (f32[3,112,256]{2,1,0:T(8,128)S(1)}, f32[3,112,256]{2,1,0:T(8,128)S(1)}, u32[]{:S(2)}, u32[]{:S(2)}) collective-permute-start(f32[3,112,256]{2,1,0:T(8,128)S(1)} %get-tuple-element.78.refs_1_.refs_0_.refs_3_.refs_5_), channel_id=1, source_target_pairs={{1,2},{2,1},{3,4},{4,3},{5,6},{6,5},{0,8},{7,15},{9,10},{10,9},{11... | collective-permute-start | bytes 1032200 | tf_op jit(solution)/shard_map/ppermute | solution.py:422
  10.1 6.8 %collective-permute-start.3 = (f32[3,48,256]{2,1,0:T(8,128)S(1)}, f32[3,48,256]{2,1,0:T(8,128)S(1)}, u32[]{:S(2)}, u32[]{:S(2)}) collective-permute-start(f32[3,48,256]{2,1,0:T(8,128)S(1)} %get-tuple-element.84.refs_2_.refs_1_.refs_6_), channel_id=1, source_target_pairs={{1,2},{2,1},{3,4},{4,3},{5,6},{6,5},{0,8},{7,15},{9,10},{10,9},{11... | collective-permute-start | bytes 442376 | tf_op jit(solution)/shard_map/ppermute | solution.py:422
  18.9 9.9 %collective-permute-start.7 = (f32[3,160,256]{2,1,0:T(8,128)S(1)}, f32[3,160,256]{2,1,0:T(8,128)S(1)}, u32[]{:S(2)}, u32[]{:S(2)}) collective-permute-start(f32[3,160,256]{2,1,0:T(8,128)S(1)} %get-tuple-element.96.refs_0_.refs_2_.refs_4_), channel_id=1, source_target_pairs={{0,1},{1,0},{2,3},{3,2},{4,5},{5,4},{6,7},{7,6},{8,9},{9,8},{10,11... | collective-permute-start | bytes 1474568 | tf_op jit(solution)/shard_map/ppermute | solution.py:425
  19.0 7.0 %collective-permute-start.2 = (f32[3,104,256]{2,1,0:T(8,128)S(1)}, f32[3,104,256]{2,1,0:T(8,128)S(1)}, u32[]{:S(2)}, u32[]{:S(2)}) collective-permute-start(f32[3,104,256]{2,1,0:T(8,128)S(1)} %get-tuple-element.87.refs_1_.refs_0_.refs_3_.refs_5_), channel_id=1, source_target_pairs={{1,2},{2,1},{3,4},{4,3},{5,6},{6,5},{0,8},{7,15},{9,10},{10,9},{11... | collective-permute-start | bytes 958472 | tf_op jit(solution)/shard_map/ppermute | solution.py:422
  21.0 6.8 %collective-permute-start.6 = (f32[3,56,256]{2,1,0:T(8,128)S(1)}, f32[3,56,256]{2,1,0:T(8,128)S(1)}, u32[]{:S(2)}, u32[]{:S(2)}) collective-permute-start(f32[3,56,256]{2,1,0:T(8,128)S(1)} %get-tuple-element.92.refs_2_.refs_1_.refs_6_), channel_id=1, source_target_pairs={{1,2},{2,1},{3,4},{4,3},{5,6},{6,5},{0,8},{7,15},{9,10},{10,9},{11... | collective-permute-start | bytes 516104 | tf_op jit(solution)/shard_map/ppermute | solution.py:422
  30.0 10.1 %collective-permute-start.10 = (f32[3,160,256]{2,1,0:T(8,128)S(1)}, f32[3,160,256]{2,1,0:T(8,128)S(1)}, u32[]{:S(2)}, u32[]{:S(2)}) collective-permute-start(f32[3,160,256]{2,1,0:T(8,128)S(1)} %get-tuple-element.104.refs_0_.refs_2_.refs_4_), channel_id=1, source_target_pairs={{0,1},{1,0},{2,3},{3,2},{4,5},{5,4},{6,7},{7,6},{8,9},{9,8},{10,11... | collective-permute-start | bytes 1474568 | tf_op jit(solution)/shard_map/ppermute | solution.py:425
  30.2 6.7 %collective-permute-start.5 = (f32[3,96,256]{2,1,0:T(8,128)S(1)}, f32[3,96,256]{2,1,0:T(8,128)S(1)}, u32[]{:S(2)}, u32[]{:S(2)}) collective-permute-start(f32[3,96,256]{2,1,0:T(8,128)S(1)} %get-tuple-element.95.refs_1_.refs_0_.refs_3_.refs_5_), channel_id=1, source_target_pairs={{1,2},{2,1},{3,4},{4,3},{5,6},{6,5},{0,8},{7,15},{9,10},{10,9},{11... | collective-permute-start | bytes 884744 | tf_op jit(solution)/shard_map/ppermute | solution.py:422
  32.1 6.8 %collective-permute-start.9 = (f32[3,64,256]{2,1,0:T(8,128)S(1)}, f32[3,64,256]{2,1,0:T(8,128)S(1)}, u32[]{:S(2)}, u32[]{:S(2)}) collective-permute-start(f32[3,64,256]{2,1,0:T(8,128)S(1)} %get-tuple-element.100.refs_2_.refs_1_.refs_6_), channel_id=1, source_target_pairs={{1,2},{2,1},{3,4},{4,3},{5,6},{6,5},{0,8},{7,15},{9,10},{10,9},{11... | collective-permute-start | bytes 589832 | tf_op jit(solution)/shard_map/ppermute | solution.py:422
  41.2 10.2 %collective-permute-start.13 = (f32[3,160,256]{2,1,0:T(8,128)S(1)}, f32[3,160,256]{2,1,0:T(8,128)S(1)}, u32[]{:S(2)}, u32[]{:S(2)}) collective-permute-start(f32[3,160,256]{2,1,0:T(8,128)S(1)} %get-tuple-element.112.refs_0_.refs_2_.refs_4_), channel_id=1, source_target_pairs={{0,1},{1,0},{2,3},{3,2},{4,5},{5,4},{6,7},{7,6},{8,9},{9,8},{10,11... | collective-permute-start | bytes 1474568 | tf_op jit(solution)/shard_map/ppermute | solution.py:425
  41.4 6.5 %collective-permute-start.8 = (f32[3,88,256]{2,1,0:T(8,128)S(1)}, f32[3,88,256]{2,1,0:T(8,128)S(1)}, u32[]{:S(2)}, u32[]{:S(2)}) collective-permute-start(f32[3,88,256]{2,1,0:T(8,128)S(1)} %get-tuple-element.103.refs_1_.refs_0_.refs_3_.refs_5_), channel_id=1, source_target_pairs={{1,2},{2,1},{3,4},{4,3},{5,6},{6,5},{0,8},{7,15},{9,10},{10,9},{11... | collective-permute-start | bytes 811016 | tf_op jit(solution)/shard_map/ppermute | solution.py:422
  43.4 6.8 %collective-permute-start.12 = (f32[3,72,256]{2,1,0:T(8,128)S(1)}, f32[3,72,256]{2,1,0:T(8,128)S(1)}, u32[]{:S(2)}, u32[]{:S(2)}) collective-permute-start(f32[3,72,256]{2,1,0:T(8,128)S(1)} %get-tuple-element.108.refs_2_.refs_1_.refs_6_), channel_id=1, source_target_pairs={{1,2},{2,1},{3,4},{4,3},{5,6},{6,5},{0,8},{7,15},{9,10},{10,9},{11... | collective-permute-start | bytes 663560 | tf_op jit(solution)/shard_map/ppermute | solution.py:422
  52.4 10.1 %collective-permute-start.16 = (f32[3,160,256]{2,1,0:T(8,128)S(1)}, f32[3,160,256]{2,1,0:T(8,128)S(1)}, u32[]{:S(2)}, u32[]{:S(2)}) collective-permute-start(f32[3,160,256]{2,1,0:T(8,128)S(1)} %get-tuple-element.120.refs_0_.refs_2_.refs_4_), channel_id=1, source_target_pairs={{0,1},{1,0},{2,3},{3,2},{4,5},{5,4},{6,7},{7,6},{8,9},{9,8},{10,11... | collective-permute-start | bytes 1474568 | tf_op jit(solution)/shard_map/ppermute | solution.py:425
  52.6 6.2 %collective-permute-start.11 = (f32[3,80,256]{2,1,0:T(8,128)S(1)}, f32[3,80,256]{2,1,0:T(8,128)S(1)}, u32[]{:S(2)}, u32[]{:S(2)}) collective-permute-start(f32[3,80,256]{2,1,0:T(8,128)S(1)} %get-tuple-element.111.refs_1_.refs_0_.refs_3_.refs_5_), channel_id=1, source_target_pairs={{1,2},{2,1},{3,4},{4,3},{5,6},{6,5},{0,8},{7,15},{9,10},{10,9},{11... | collective-permute-start | bytes 737288 | tf_op jit(solution)/shard_map/ppermute | solution.py:422
  54.6 6.8 %collective-permute-start.15 = (f32[3,80,256]{2,1,0:T(8,128)S(1)}, f32[3,80,256]{2,1,0:T(8,128)S(1)}, u32[]{:S(2)}, u32[]{:S(2)}) collective-permute-start(f32[3,80,256]{2,1,0:T(8,128)S(1)} %get-tuple-element.116.refs_2_.refs_1_.refs_6_), channel_id=1, source_target_pairs={{1,2},{2,1},{3,4},{4,3},{5,6},{6,5},{0,8},{7,15},{9,10},{10,9},{11... | collective-permute-start | bytes 737288 | tf_op jit(solution)/shard_map/ppermute | solution.py:422
  63.7 12.7 %collective-permute-start.19 = (f32[3,160,256]{2,1,0:T(8,128)S(1)}, f32[3,160,256]{2,1,0:T(8,128)S(1)}, u32[]{:S(2)}, u32[]{:S(2)}) collective-permute-start(f32[3,160,256]{2,1,0:T(8,128)S(1)} %get-tuple-element.128.refs_0_.refs_2_.refs_4_), channel_id=1, source_target_pairs={{0,1},{1,0},{2,3},{3,2},{4,5},{5,4},{6,7},{7,6},{8,9},{9,8},{10,11... | collective-permute-start | bytes 1474568 | tf_op jit(solution)/shard_map/ppermute | solution.py:425
  63.9 9.4 %collective-permute-start.18 = (f32[3,88,256]{2,1,0:T(8,128)S(1)}, f32[3,88,256]{2,1,0:T(8,128)S(1)}, u32[]{:S(2)}, u32[]{:S(2)}) collective-permute-start(f32[3,88,256]{2,1,0:T(8,128)S(1)} %get-tuple-element.124.refs_2_.refs_1_.refs_6_), channel_id=1, source_target_pairs={{1,2},{2,1},{3,4},{4,3},{5,6},{6,5},{0,8},{7,15},{9,10},{10,9},{11... | collective-permute-start | bytes 811016 | tf_op jit(solution)/shard_map/ppermute | solution.py:422
  65.9 6.8 %collective-permute-start.14 = (f32[3,72,256]{2,1,0:T(8,128)S(1)}, f32[3,72,256]{2,1,0:T(8,128)S(1)}, u32[]{:S(2)}, u32[]{:S(2)}) collective-permute-start(f32[3,72,256]{2,1,0:T(8,128)S(1)} %get-tuple-element.119.refs_1_.refs_0_.refs_3_.refs_5_), channel_id=1, source_target_pairs={{1,2},{2,1},{3,4},{4,3},{5,6},{6,5},{0,8},{7,15},{9,10},{10,9},{11... | collective-permute-start | bytes 663560 | tf_op jit(solution)/shard_map/ppermute | solution.py:422
  74.4 9.3 %collective-permute-start.21 = (f32[3,96,256]{2,1,0:T(8,128)S(1)}, f32[3,96,256]{2,1,0:T(8,128)S(1)}, u32[]{:S(2)}, u32[]{:S(2)}) collective-permute-start(f32[3,96,256]{2,1,0:T(8,128)S(1)} %get-tuple-element.132.refs_2_.refs_1_.refs_6_), channel_id=1, source_target_pairs={{1,2},{2,1},{3,4},{4,3},{5,6},{6,5},{0,8},{7,15},{9,10},{10,9},{11... | collective-permute-start | bytes 884744 | tf_op jit(solution)/shard_map/ppermute | solution.py:422
  76.4 6.8 %collective-permute-start.17 = (f32[3,64,256]{2,1,0:T(8,128)S(1)}, f32[3,64,256]{2,1,0:T(8,128)S(1)}, u32[]{:S(2)}, u32[]{:S(2)}) collective-permute-start(f32[3,64,256]{2,1,0:T(8,128)S(1)} %get-tuple-element.127.refs_1_.refs_0_.refs_3_.refs_5_), channel_id=1, source_target_pairs={{1,2},{2,1},{3,4},{4,3},{5,6},{6,5},{0,8},{7,15},{9,10},{10,9},{11... | collective-permute-start | bytes 589832 | tf_op jit(solution)/shard_map/ppermute | solution.py:422
  77.6 10.0 %collective-permute-start.22 = (f32[3,160,256]{2,1,0:T(8,128)S(1)}, f32[3,160,256]{2,1,0:T(8,128)S(1)}, u32[]{:S(2)}, u32[]{:S(2)}) collective-permute-start(f32[3,160,256]{2,1,0:T(8,128)S(1)} %get-tuple-element.136.refs_0_.refs_2_.refs_4_), channel_id=1, source_target_pairs={{0,1},{1,0},{2,3},{3,2},{4,5},{5,4},{6,7},{7,6},{8,9},{9,8},{10,11... | collective-permute-start | bytes 1474568 | tf_op jit(solution)/shard_map/ppermute | solution.py:425
  83.6 3.4 %copy-start.1 = (f32[4,2,160,256]{3,2,1,0:T(8,128)S(1)}, f32[4,2,160,256]{3,2,1,0:T(8,128)}, u32[]{:S(2)}) copy-start(f32[4,2,160,256]{3,2,1,0:T(8,128)} %s.7) | copy-start | bytes 3932164
  83.7 3.4 %copy-start.2 = (f32[4,2,160,256]{3,2,1,0:T(8,128)S(1)}, f32[4,2,160,256]{3,2,1,0:T(8,128)}, u32[]{:S(2)}) copy-start(f32[4,2,160,256]{3,2,1,0:T(8,128)} %y.7) | copy-start | bytes 3932164
  85.0 10.1 %collective-permute-start.23 = (f32[3,104,256]{2,1,0:T(8,128)S(1)}, f32[3,104,256]{2,1,0:T(8,128)S(1)}, u32[]{:S(2)}, u32[]{:S(2)}) collective-permute-start(f32[3,104,256]{2,1,0:T(8,128)S(1)} %get-tuple-element.140.refs_2_.refs_1_), channel_id=1, source_target_pairs={{1,2},{2,1},{3,4},{4,3},{5,6},{6,5},{0,8},{7,15},{9,10},{10,9},{11... | collective-permute-start | bytes 958472 | tf_op jit(solution)/shard_map/ppermute | solution.py:422
  87.0 6.8 %collective-permute-start.20 = (f32[3,56,256]{2,1,0:T(8,128)S(1)}, f32[3,56,256]{2,1,0:T(8,128)S(1)}, u32[]{:S(2)}, u32[]{:S(2)}) collective-permute-start(f32[3,56,256]{2,1,0:T(8,128)S(1)} %get-tuple-element.135.refs_1_.refs_0_), channel_id=1, source_target_pairs={{1,2},{2,1},{3,4},{4,3},{5,6},{6,5},{0,8},{7,15},{9,10},{10,9},{11... | collective-permute-start | bytes 516104 | tf_op jit(solution)/shard_map/ppermute | solution.py:422
  96.6 1.2 %collective-permute-start.24 = (f32[32,128]{1,0:T(8,128)S(1)}, f32[32,128]{1,0:T(8,128)S(1)}, u32[]{:S(2)}, u32[]{:S(2)}) collective-permute-start(f32[32,128]{1,0:T(8,128)S(1)} %shard_map.151), channel_id=1, source_target_pairs={{0,1},{1,0},{2,3},{3,2},{4,5},{5,4},{6,7},{7,6},{8,9},{9,8},{10,11... | collective-permute-start | bytes 49160 | tf_op jit(solution)/shard_map/ppermute | solution.py:385
  97.9 5.5 %collective-permute-start.25 = (f32[32,128]{1,0:T(8,128)S(1)}, f32[32,128]{1,0:T(8,128)S(1)}, u32[]{:S(2)}, u32[]{:S(2)}) collective-permute-start(f32[32,128]{1,0:T(8,128)S(1)} %add.3), channel_id=1, source_target_pairs={{0,2},{1,3},{2,4},{3,5},{4,6},{5,7},{6,0},{7,1},{8,10},{9,11},{10,... | collective-permute-start | bytes 49160 | tf_op jit(solution)/shard_map/ppermute | solution.py:390
  97.9 5.5 %collective-permute-start.26 = (f32[32,128]{1,0:T(8,128)S(1)}, f32[32,128]{1,0:T(8,128)S(1)}, u32[]{:S(2)}, u32[]{:S(2)}) collective-permute-start(f32[32,128]{1,0:T(8,128)S(1)} %add.3), channel_id=1, source_target_pairs={{0,4},{1,5},{2,6},{3,7},{4,0},{5,1},{6,2},{7,3},{8,12},{9,13},{10,... | collective-permute-start | bytes 49160 | tf_op jit(solution)/shard_map/ppermute | solution.py:390
  97.9 6.0 %collective-permute-start.27 = (f32[32,128]{1,0:T(8,128)S(1)}, f32[32,128]{1,0:T(8,128)S(1)}, u32[]{:S(2)}, u32[]{:S(2)}) collective-permute-start(f32[32,128]{1,0:T(8,128)S(1)} %add.3), channel_id=1, source_target_pairs={{0,6},{1,7},{2,0},{3,1},{4,2},{5,3},{6,4},{7,5},{8,14},{9,15},{10,... | collective-permute-start | bytes 49160 | tf_op jit(solution)/shard_map/ppermute | solution.py:390
  (7 other events, 8.7 us)
